TPU v7x, 256 devices: a 8x8x2 block of a 8x8x16 slice. The times are simulated.
256 devices in a mesh: grp: 2 (over z), scen: 128 (over x, y, core).
Axes of the slice: x: 8, y: 8, z: 2, core: 2. Of those that a mesh axis runs over, the one named last changes fastest.
The devices are a block of a 8x8x16 slice.
Arguments:
- shocks: bfloat16 [262144, 2048], P(('grp', 'scen')), parts along dimension 0, may hold values from -8 to 8
- factor_sens: bfloat16 [2048, 1024], replicated, may hold values from -0.13258252 to 0.13258252
- notional: float32 [1024], replicated, may hold values from -0.25 to 0.25
- moneyness: float32 [1024], replicated, may hold values from -2 to 2
- desk_entity: int32 [64], replicated, may hold values from 0 to 7
- scenario_counts: int32 [256], P(('grp', 'scen')), parts along dimension 0, may hold values from 256 to 1024, as said below
- candidate_ids: int32 [2048], P('grp'), parts along dimension 0, may hold values from 0 to 131071, as said below
Outputs:
- tail_losses: float32 [512], P('grp'), parts along dimension 0
- cand_entity: float32 [2048, 8], P(('grp', 'scen')), parts along dimension 0
There are 2 independent parts, one for each index of `grp`. A program takes and returns all parts, laid end to end along the dimension named above; an argument that names none is the same for every part. Nothing has to cross between parts.
Inputs may be any that keep to these rules, and one draw needn't show every extreme that they name: `scenario_counts`: every block has at least 256 valid scenarios; some block in every draw is full. `candidate_ids`: each id b * 1024 + j names a valid scenario: j is below scenario_counts[b].
All inputs are finite; a program needn't handle non-finite values.
Results may differ from a plain program's by a relative error of at most 0.0003.
Values sent between devices are 32-bit elements; how exact they have to be, the bound alone decides.
A program may use at most 128 MiB of HBM per device.

v0:
```python
import jax
import jax.numpy as jnp
from jax import lax
from jax.sharding import Mesh
from jax.sharding import PartitionSpec as P

K = 64
INSTR = 16
ENT = 8
TOPK = 256
SCEN = ("scen_0", "scen_1", "scen_2")
GRP_SCEN = ("grp", "scen_0", "scen_1", "scen_2")


def sent_to_all(array, axis):
    devices = lax.axis_size(axis)
    return lax.all_to_all(
        jnp.broadcast_to(array[None], (devices, *array.shape)), axis, 0, 0, tiled=True
    )


def joined_along(blocks, dim):
    dims = list(blocks.shape[1:])
    dims[dim] *= blocks.shape[0]
    return jnp.moveaxis(blocks, 0, dim).reshape(dims)


def whole_of(array, axes, dim):
    far, near = axes
    leading = sent_to_all(array, far)
    blocks = jnp.swapaxes(sent_to_all(leading, near), 0, 1)
    return joined_along(blocks.reshape(-1, *array.shape), dim)


def in_blocks(array, dim, devices):
    before, after = (array.shape[:dim], array.shape[dim + 1 :])
    return jnp.moveaxis(array.reshape(*before, devices, -1, *after), dim, 0)


def sent_and_summed(array, axis, dim):
    devices = lax.axis_size(axis)
    blocks = lax.all_to_all(in_blocks(array, dim, devices), axis, 0, 0, tiled=True)
    return jnp.sum(blocks, axis=0)


def sum_in_two_steps(array, axes, dim):
    far, near = axes
    own = sent_and_summed(in_blocks(array, dim, lax.axis_size(far)), near, dim + 1)
    return jnp.sum(lax.all_to_all(own, far, 0, 0, tiled=True), axis=0)


def price(rows, factor_sens, notional, moneyness):
    value = jnp.dot(rows, factor_sens, preferred_element_type=jnp.float32)
    inst = notional * (jax.nn.softplus(value + moneyness) - jax.nn.softplus(moneyness))
    return jnp.sum(inst.reshape(rows.shape[0], K, INSTR), axis=2)


def body(shocks, factor_sens, notional, moneyness, desk_entity, scenario_counts, candidate_ids):
    slots = shocks.shape[0]
    count = scenario_counts[0]
    block_rows = min(256, slots)
    turns = slots // block_rows

    def one_block(step, desk_all):
        start = step * block_rows

        def active(unused):
            rows = lax.dynamic_slice_in_dim(shocks, start, block_rows, 0)
            return price(rows, factor_sens, notional, moneyness)

        def skipped(unused):
            return jnp.zeros((block_rows, K), jnp.float32)

        piece = lax.cond(start < count, active, skipped, 0)
        return lax.dynamic_update_slice_in_dim(desk_all, piece, start, 0)

    desk_pnl = lax.fori_loop(0, turns, one_block, jnp.zeros((slots, K), jnp.float32))
    loss = -jnp.sum(desk_pnl, axis=1)
    valid = jnp.arange(slots, dtype=jnp.int32) < count
    local_top = lax.top_k(jnp.where(valid, loss, jnp.float32(-1e30)), TOPK)[0]
    every_list = whole_of(local_top, (("scen_0", "scen_1"), "scen_2"), 0)
    tail_losses = lax.top_k(every_list, TOPK)[0]
    local_ids = candidate_ids - lax.axis_index(SCEN) * slots
    owned = (local_ids >= 0) & (local_ids < slots)
    clipped = jnp.clip(local_ids, 0, slots - 1)
    onehot = (desk_entity[:, None] == jnp.arange(ENT, dtype=jnp.int32)[None, :]).astype(jnp.float32)
    cand_pnl = sum_in_two_steps(
        jnp.where(owned[:, None], jnp.take(desk_pnl, clipped, axis=0), jnp.float32(0.0)),
        (("scen_0", "scen_1"), "scen_2"),
        0,
    )
    cand_entity = -jnp.dot(cand_pnl, onehot, precision=lax.Precision.HIGHEST)
    return (tail_losses, cand_entity)


def solution(mesh):
    finer = Mesh(
        mesh.devices.reshape(mesh.shape["grp"], 8, 8, 2), ("grp", "scen_0", "scen_1", "scen_2")
    )
    return jax.shard_map(
        body,
        mesh=finer,
        in_specs=(P(GRP_SCEN, None), P(), P(), P(), P(), P(GRP_SCEN), P("grp")),
        out_specs=(P("grp"), P(GRP_SCEN, None)),
        check_vma=False,
    )
```

profile of v0, /device:TPU:513, one launch (start us, length us, event | category | flops | bytes accessed | tf_op | source)
XLA Modules:
  0.0 100.6 jit_solution(2023195208638861984)
XLA Ops:
  0.6 0.7 fusion.7
  1.3 0.7 compare_and_fusion.1
  2.1 25.0 %while.13 = (s32[]{:T(128)}, f32[1024,64]{0,1:T(8,128)S(1)}, s32[]{:T(128)}, f32[1024]{0:T(1024)}, bf16[1024,2048]{1,0:T(8,128)(2,1)}, /*index=5*/bf16[2048,1024...) while((s32[]{:T(128)}, f32[1024,64]{0,1:T(8,128)S(1)}, ...), condition=%wide.region_4.5_spmd, body=%wide.region_0.4_spmd.sunk | while | flops 1076353024 | bytes 9654539 | solution.py:77
  2.7 5.6 %conditional.2 = (f32[256,64]{0,1:T(8,128)S(1)}) conditional(s32[]{:T(128)} %convert_element_type.9, () %tuple.41, (f32[1024]{0:T(1024)}, s32[]{:T(128)}, bf16[1024,2048]{1,0:T(8,128)(2,1)}, bf16[2048,1024]{1,0:T(8,128)(2,1)}, f32[1024]{0:T(1024)}) %tuple.42), branch_computations={%region_1.0_spmd, %region_2.3_spmd} | conditional | flops 1076353024 | bytes 9523246 | solution.py:74
  2.7 0.7 compare_select_fusion.1
  3.4 4.3 %fusion.1 = f32[256,1024]{1,0:T(8,128)S(1)} fusion(bf16[2048,1024]{1,0:T(8,128)(2,1)} %get-tuple-element.137, bf16[1024,2048]{1,0:T(8,128)(2,1)} %get-tuple-element.135, s32[]{:T(128)S(6)} %select_n.29, f32[1024]{0:T(1024)S(1)} %compare_select_fusion.1, f32[1024]{0:T(1024)} %get-tuple-element.138, f32[1024]{0:T(1024)} %get-tuple-element.134), kind=kOutput, calls=%fused_computation.4 | convolution fusion | flops 1076101120 | bytes 6303748 | tf_op jit(solution)/shard_map/while/body/eval_jaxpr/cond/branch_1_fun/dot_general | solution.py:53
  9.0 5.6 %conditional.2 = (f32[256,64]{0,1:T(8,128)S(1)}) conditional(s32[]{:T(128)} %convert_element_type.9, () %tuple.41, (f32[1024]{0:T(1024)}, s32[]{:T(128)}, bf16[1024,2048]{1,0:T(8,128)(2,1)}, bf16[2048,1024]{1,0:T(8,128)(2,1)}, f32[1024]{0:T(1024)}) %tuple.42), branch_computations={%region_1.0_spmd, %region_2.3_spmd} | conditional | flops 1076353024 | bytes 9523246 | solution.py:74
  9.0 0.7 compare_select_fusion.1
  9.7 4.3 %fusion.1 = f32[256,1024]{1,0:T(8,128)S(1)} fusion(bf16[2048,1024]{1,0:T(8,128)(2,1)} %get-tuple-element.137, bf16[1024,2048]{1,0:T(8,128)(2,1)} %get-tuple-element.135, s32[]{:T(128)S(6)} %select_n.29, f32[1024]{0:T(1024)S(1)} %compare_select_fusion.1, f32[1024]{0:T(1024)} %get-tuple-element.138, f32[1024]{0:T(1024)} %get-tuple-element.134), kind=kOutput, calls=%fused_computation.4 | convolution fusion | flops 1076101120 | bytes 6303748 | tf_op jit(solution)/shard_map/while/body/eval_jaxpr/cond/branch_1_fun/dot_general | solution.py:53
  15.2 5.6 %conditional.2 = (f32[256,64]{0,1:T(8,128)S(1)}) conditional(s32[]{:T(128)} %convert_element_type.9, () %tuple.41, (f32[1024]{0:T(1024)}, s32[]{:T(128)}, bf16[1024,2048]{1,0:T(8,128)(2,1)}, bf16[2048,1024]{1,0:T(8,128)(2,1)}, f32[1024]{0:T(1024)}) %tuple.42), branch_computations={%region_1.0_spmd, %region_2.3_spmd} | conditional | flops 1076353024 | bytes 9523246 | solution.py:74
  15.3 0.7 compare_select_fusion.1
  16.0 4.3 %fusion.1 = f32[256,1024]{1,0:T(8,128)S(1)} fusion(bf16[2048,1024]{1,0:T(8,128)(2,1)} %get-tuple-element.137, bf16[1024,2048]{1,0:T(8,128)(2,1)} %get-tuple-element.135, s32[]{:T(128)S(6)} %select_n.29, f32[1024]{0:T(1024)S(1)} %compare_select_fusion.1, f32[1024]{0:T(1024)} %get-tuple-element.138, f32[1024]{0:T(1024)} %get-tuple-element.134), kind=kOutput, calls=%fused_computation.4 | convolution fusion | flops 1076101120 | bytes 6303748 | tf_op jit(solution)/shard_map/while/body/eval_jaxpr/cond/branch_1_fun/dot_general | solution.py:53
  21.5 5.6 %conditional.2 = (f32[256,64]{0,1:T(8,128)S(1)}) conditional(s32[]{:T(128)} %convert_element_type.9, () %tuple.41, (f32[1024]{0:T(1024)}, s32[]{:T(128)}, bf16[1024,2048]{1,0:T(8,128)(2,1)}, bf16[2048,1024]{1,0:T(8,128)(2,1)}, f32[1024]{0:T(1024)}) %tuple.42), branch_computations={%region_1.0_spmd, %region_2.3_spmd} | conditional | flops 1076353024 | bytes 9523246 | solution.py:74
  21.5 0.7 compare_select_fusion.1
  22.2 4.3 %fusion.1 = f32[256,1024]{1,0:T(8,128)S(1)} fusion(bf16[2048,1024]{1,0:T(8,128)(2,1)} %get-tuple-element.137, bf16[1024,2048]{1,0:T(8,128)(2,1)} %get-tuple-element.135, s32[]{:T(128)S(6)} %select_n.29, f32[1024]{0:T(1024)S(1)} %compare_select_fusion.1, f32[1024]{0:T(1024)} %get-tuple-element.138, f32[1024]{0:T(1024)} %get-tuple-element.134), kind=kOutput, calls=%fused_computation.4 | convolution fusion | flops 1076101120 | bytes 6303748 | tf_op jit(solution)/shard_map/while/body/eval_jaxpr/cond/branch_1_fun/dot_general | solution.py:53
  27.6 2.8 %gather_fusion = f32[1024,64]{1,0:T(8,128)S(1)} fusion(f32[1024,64]{1,0:T(8,128)S(1)} %copy.20, s32[1024]{0:T(1024)S(1)} %fusion.7), kind=kCustom, calls=%fused_computation | custom fusion | bytes 528384 | tf_op jit(solution)/shard_map/jit(_take)/gather | solution.py:88
  30.8 1.0 %reshape.45 = f32[2,1,32768]{2,1,0:T(1,128)} reshape(f32[2,64,8,64]{3,2,1,0:T(8,128)S(1)} %fusion.5) | data formatting | bytes 524288
  31.8 18.3 %all-to-all-start.2 = ((f32[2,1,32768]{2,1,0:T(1,128)}), f32[2,1,32768]{2,1,0:T(1,128)S(1)}, u32[]{:S(2)}, u32[]{:S(2)}) async-start(f32[2,1,32768]{2,1,0:T(1,128)} %reshape.45), calls=%async_computation.2 | async-start | bytes 524288 | tf_op jit(solution)/shard_map/all_to_all | solution.py:42
  50.8 4.4 %top_k.14 = (f32[1024]{0:T(1024)S(1)}, s32[1024]{0:T(1024)}) sort(f32[1024]{0:T(1024)S(1)} %negate_select_fusion, s32[1024]{0:T(1024)S(1)} %iota.14), dimensions={0}, to_apply=%region_6.7 | sort | flops 10240 | bytes 16384 | tf_op jit(solution)/shard_map/top_k | solution.py:80
  55.2 0.7 broadcast_in_dim.57
  55.9 6.7 %all-to-all-start = ((f32[64,1,256]{2,1,0:T(1,128)}), f32[64,1,256]{2,1,0:T(1,128)S(1)}, u32[]{:S(2)}, u32[]{:S(2)}) async-start(f32[64,1,256]{2,1,0:T(1,128)} %broadcast_in_dim.57), calls=%async_computation | async-start | bytes 131072 | tf_op jit(solution)/shard_map/all_to_all | solution.py:17
  62.6 0.5 broadcast.28
  63.1 1.4 %reduce = f32[2,32768]{1,0:T(2,128)S(1)} reduce(f32[2,1,32768]{2,1,0:T(1,128)S(1)} %all-to-all-done.2, f32[]{:T(128)} %broadcast.28), dimensions={1}, to_apply=%all_to_all.15.reduce_sub_computation | reduce | bytes 524292 | tf_op jit(solution)/shard_map/all_to_all | solution.py:42
  64.6 0.3 reshape.46
  65.0 0.8 reshape.47
  65.8 6.7 %all-to-all-done = f32[64,1,256]{2,1,0:T(1,128)S(1)} async-done(((f32[64,1,256]{2,1,0:T(1,128)}), f32[64,1,256]{2,1,0:T(1,128)S(1)}, u32[]{:S(2)}, u32[]{:S(2)}) %all-to-all-start) | async-done | bytes 65568 | tf_op jit(solution)/shard_map/all_to_all | solution.py:17
  72.5 4.9 %all_to_all.21 = f32[2,64,256]{2,1,0:T(8,128)S(1)} all-to-all(f32[2,64,256]{2,1,0:T(8,128)S(1)} %broadcast_in_dim.59), channel_id=1, replica_groups=mesh['grp'=2,'scen_0'=8,'scen_1'=8,'scen_2'=2] {'scen_2'}, dimensions={0} | all-to-all | bytes 262144 | tf_op jit(solution)/shard_map/all_to_all | solution.py:17
  77.5 6.7 %all-to-all-start.3 = ((f32[64,1,512]{2,1,0:T(1,128)}), f32[64,1,512]{2,1,0:T(1,128)S(1)}, u32[]{:S(2)}, u32[]{:S(2)}) async-start(f32[64,1,512]{2,1,0:T(1,128)} %reshape.47), calls=%async_computation.3 | async-start | bytes 262144 | tf_op jit(solution)/shard_map/all_to_all | solution.py:49
  84.3 13.8 %top_k.20 = (f32[32768]{0:T(1024)S(1)}, s32[32768]{0:T(1024)}) sort(f32[32768]{0:T(1024)S(1)} %bitcast.19, s32[32768]{0:T(1024)S(1)} %iota.15), dimensions={0}, to_apply=%region_7.8 | sort | flops 491520 | bytes 524288 | tf_op jit(solution)/shard_map/top_k | solution.py:82
  98.1 0.6 top_k.21
  98.7 1.0 reduce.1
  99.8 0.8 convolution_negate_fusion
  (35 shorter events, 3.4 us)
Async XLA Ops:
  30.4 69.4 %copy-start = (s32[64]{0:T(128)S(1)}, s32[64]{0:T(128)}, u32[]{:S(2)}) copy-start(s32[64]{0:T(128)} %param.15) | copy-start | bytes 772
  31.8 23.4 %all-to-all-start.2 = ((f32[2,1,32768]{2,1,0:T(1,128)}), f32[2,1,32768]{2,1,0:T(1,128)S(1)}, u32[]{:S(2)}, u32[]{:S(2)}) async-start(f32[2,1,32768]{2,1,0:T(1,128)} %reshape.45), calls=%async_computation.2 | async-start | bytes 524288 | tf_op jit(solution)/shard_map/all_to_all | solution.py:42
  55.9 16.6 %all-to-all-start = ((f32[64,1,256]{2,1,0:T(1,128)}), f32[64,1,256]{2,1,0:T(1,128)S(1)}, u32[]{:S(2)}, u32[]{:S(2)}) async-start(f32[64,1,256]{2,1,0:T(1,128)} %broadcast_in_dim.57), calls=%async_computation | async-start | bytes 131072 | tf_op jit(solution)/shard_map/all_to_all | solution.py:17
  77.5 21.2 %all-to-all-start.3 = ((f32[64,1,512]{2,1,0:T(1,128)}), f32[64,1,512]{2,1,0:T(1,128)S(1)}, u32[]{:S(2)}, u32[]{:S(2)}) async-start(f32[64,1,512]{2,1,0:T(1,128)} %reshape.47), calls=%async_computation.3 | async-start | bytes 262144 | tf_op jit(solution)/shard_map/all_to_all | solution.py:49
where the time goes:
time: 102 us; the launch traced here: 101 us
  starting transfers between devices  31.7 us (31%)
  other arithmetic  26 us (25%)
  matrix products  18 us (18%)
  local copies, waits for them, and re-layouts  8.88 us (9%)
  waiting for transfers between devices  6.72 us (7%)
  blocking collectives  4.95 us (5%)
  loops' own time  2.9 us (3%)
  between operations  1.45 us (1%)
    all_to_all x1, starting transfers between devices, sent_and_summed(): lax.all_to_all(in_blocks(array, dim, devices), axis, 0, 0, tiled=True)  18.3 us
    dot_general x4, matrix products, price(): value = jnp.dot(rows, factor_sens, preferred_element_type=jnp.float32)  17.2 us
    top_k x1, other arithmetic, body(): tail_losses = lax.top_k(every_list, TOPK)[0]  13.8 us
    all_to_all x1, waiting for transfers between devices, sent_to_all(): lax.all_to_all(jnp.broadcast_to(array[None], (devices, *array.shape)), ax...  6.71 us
    all_to_all x1, starting transfers between devices, sent_to_all(): lax.all_to_all(jnp.broadcast_to(array[None], (devices, *array.shape)), ax...  6.7 us
    all_to_all x1, starting transfers between devices, sum_in_two_steps(): return jnp.sum(lax.all_to_all(own, far, 0, 0, tiled=True), axis=0)  6.66 us
    all_to_all x1, blocking collectives, sent_to_all(): lax.all_to_all(jnp.broadcast_to(array[None], (devices, *array.shape)), ax...  4.95 us
    top_k x1, other arithmetic, body(): local_top = lax.top_k(jnp.where(valid, loss, jnp.float32(-1e+30)), TOPK)[0]  4.43 us
  transfers between devices with their start and end apart: 3, of which 1 were waited for; matrix products, arithmetic and copies ran while one was open for 22% of the time, Pallas kernels for 0%

commit v1 on v0

v1 whole, which is shorter than its diff:
```python
import functools

import jax
import jax.numpy as jnp
from jax import lax
from jax.experimental import pallas as pl
from jax.experimental.pallas import tpu as pltpu
from jax.sharding import PartitionSpec as P

K = 64
INSTR = 16
ENT = 8
TOPK = 256
SIDE = 8
CORES = 2
LANES = 128
SUB = 8
TILE = 256
FLOOR = -1e30
MESH = pl.DeviceIdType.MESH
F32 = jnp.float32
BF16 = jnp.bfloat16


def iota(shape, dim):
    return lax.broadcasted_iota(jnp.int32, shape, dim)


def pieces(array, count):
    out = []
    for _ in range(count):
        part = array.astype(BF16).astype(F32)
        out.append(part)
        array = array - part
    return out


def pair_sum(left, right, step):
    low = (iota(left.shape, 1) & step) == 0
    up = left + pltpu.roll(left, LANES - step, 1)
    down = right + pltpu.roll(right, step, 1)
    return jnp.where(low, up, down)


def merge(stored, own, step, after):
    value = stored * own
    x = jnp.maximum(value, pltpu.roll(value, step, 1)) * after
    for stride in (128, 64, 32, 16, 8):
        y = x.reshape(TOPK // (2 * stride), 2, stride, LANES)
        a, b = y[:, 0], y[:, 1]
        x = jnp.stack([jnp.maximum(a, b), jnp.minimum(a, b)], axis=1).reshape(TOPK, LANES)
    y = x.reshape(TOPK // SUB, SUB, LANES)
    at = iota(y.shape, 1)
    for stride in (4, 2, 1):
        low = (at & stride) == 0
        if stride == 4:
            other = pltpu.roll(y, 4, 1)
        else:
            other = jnp.where(low, pltpu.roll(y, SUB - stride, 1), pltpu.roll(y, stride, 1))
        y = jnp.where(low, jnp.maximum(y, other), jnp.minimum(y, other))
    return y.reshape(TOPK, LANES)


def lists_down(rows):
    copies = LANES // rows.shape[0]
    return jnp.concatenate([rows] * copies, axis=0).T


def along_lanes(column):
    same = iota(column.shape, 0) == iota(column.shape, 1)
    return jnp.sum(jnp.where(same, column, 0.0), axis=0, keepdims=True)


def sign_of(bit):
    return jnp.where(bit, F32(-1.0), F32(1.0))


def kernel(
    shocks, sens, notional, moneyness, desk_entity, counts, ids,
    tail_out, cand_out,
    sh, fs, nv, mv, dv, cv, iv, indicator, column, spread, gathered,
    list1, list2, got1, got2, cand1, cand2, cgot1, cgot2, flipped,
    load_sem, small_sem, send1, recv1, send2, recv2, csend1, crecv1, csend2, crecv2,
):
    slots = sh.shape[0]
    turns = slots // TILE
    chunks = sens.shape[1] // TILE
    me = lax.axis_index("scen")
    x, yc = me // (SIDE * CORES), me % (SIDE * CORES)
    half = SIDE * CORES
    across = [lax.rem(x + d, SIDE) for d in range(1, SIDE)]
    along = [lax.rem(yc + d, half) for d in range(1, half)]

    def load_rows(r):
        rows = pl.ds(r * TILE, TILE)
        return pltpu.make_async_copy(shocks.at[rows], sh.at[rows], load_sem.at[r])

    def load_columns(c):
        cols = pl.ds(c * TILE, TILE)
        return pltpu.make_async_copy(sens.at[:, cols], fs.at[:, cols], load_sem.at[turns + c])

    small = [
        pltpu.make_async_copy(src, dst, small_sem.at[n])
        for n, (src, dst) in enumerate(
            [(moneyness, mv), (notional, nv), (desk_entity, dv), (counts, cv), (ids, iv)]
        )
    ]
    load_rows(0).start()
    load_columns(0).start()
    for copy in small:
        copy.start()
    for c in range(1, chunks):
        load_columns(c).start()
    for r in range(1, turns):
        load_rows(r).start()

    barrier = pltpu.get_barrier_semaphore()
    for other in across:
        pl.semaphore_signal(barrier, inc=1, device_id={"scen": other * half + yc}, device_id_type=MESH)
    for other in along:
        pl.semaphore_signal(barrier, inc=1, device_id={"scen": x * half + other}, device_id_type=MESH)

    for copy in small:
        copy.wait()

    lane = iota((TILE, LANES), 0)
    within = lane % LANES
    desk = 8 * (4 * (lane // LANES) + 2 * ((within // 4) % 2) + (within // 8) % 2) + within // 16
    place = jnp.where(desk == iota((TILE, LANES), 1), 1.0, 0.0).astype(BF16)
    entity = jnp.concatenate([dv[...], jnp.full((1, LANES - K), -1, jnp.int32)], axis=1)
    row = iota((TILE, LANES), 0)
    member = jnp.where(row < ENT, row, jnp.where(row >= LANES, -2, -3))
    hit = (entity == member) | ((member == -2) & (iota((TILE, LANES), 1) < K))
    owner = jnp.where(hit, -1.0, 0.0).astype(BF16)
    indicator[...] = lax.dot_general(
        place, owner, (((1,), (1,)), ((), ())), preferred_element_type=F32
    ).astype(BF16)
    gathered[...] = jnp.zeros(gathered.shape, F32)
    base = me * slots
    count = cv[0]

    def turn(r, first):
        load_rows(r).wait()
        rows = sh[pl.ds(r * TILE, TILE), :]
        sums = []
        for c in range(chunks):
            if first:
                load_columns(c).wait()
            value = jnp.dot(rows, fs[:, c * TILE:(c + 1) * TILE], preferred_element_type=F32)
            halves = []
            for h in range(2):
                b = 2 * c + h
                m = mv[b:b + 1, :]
                start = jnp.maximum(m, 0.0) + jnp.log(1.0 + jnp.exp(-jnp.abs(m)))
                v = value[:, h * LANES:(h + 1) * LANES] + m
                soft = jnp.maximum(v, 0.0) + jnp.log(1.0 + jnp.exp(-jnp.abs(v)))
                halves.append(nv[b:b + 1, :] * (soft - start))
            sums.append(pair_sum(halves[0], halves[1], 8))
        parts = jnp.concatenate(
            [pair_sum(sums[0], sums[1], 4), pair_sum(sums[2], sums[3], 4)], axis=1
        )
        total = jnp.zeros((TILE, TILE), F32)
        for part in pieces(parts, 3):
            total += jnp.dot(part.astype(BF16), indicator[...], preferred_element_type=F32)
        here = r * TILE + iota((TILE, LANES), 0)
        loss = jnp.where(here < count, total[:, LANES:], FLOOR)
        column[pl.ds(r * TILE, TILE), :] = loss
        for h in range(2):
            spread[2 * r + h] = loss[h * LANES:(h + 1) * LANES].T[0:SUB]
        by_entity = total[:, :LANES].T[0:ENT]
        left = jnp.concatenate(pieces(by_entity, 3), axis=0).astype(BF16)
        wanted = jnp.concatenate(
            [
                jnp.where(iv[b:b + 1, :] - base == here, 1.0, 0.0).astype(BF16)
                for b in range(SIDE)
            ],
            axis=1,
        )
        gathered[...] += jnp.dot(left, wanted, preferred_element_type=F32)

    turn(0, True)

    @pl.loop(1, turns)
    def _(r):
        turn(r, False)

    blocks = slots // LANES
    groups = slots // SUB
    level = []
    for i in range(blocks):
        mine = column[i * LANES:(i + 1) * LANES, :].reshape(LANES // SUB, SUB, LANES)
        seen = jnp.zeros(mine.shape, F32)
        for b in range(blocks):
            theirs = spread[b][None]
            if b < i:
                ahead = theirs >= mine
            elif b > i:
                ahead = theirs > mine
            else:
                own = iota(mine.shape, 0) * SUB + iota(mine.shape, 1)
                ahead = (theirs > mine) | ((theirs == mine) & (iota(mine.shape, 2) < own))
            seen = jnp.where(ahead, seen + 1.0, seen)
        level.append(seen.reshape(LANES, LANES))
    seen = jnp.concatenate(level, axis=0).astype(BF16)
    rank = jnp.dot(seen, jnp.ones((LANES, LANES), BF16), preferred_element_type=F32)

    rising1 = x >= SIDE // 2
    sign1 = sign_of(rising1)
    local = []
    for h in range(2):
        target = iota((1, LANES), 1).astype(F32) + float(h * LANES)
        target = jnp.where(rising1, float(TOPK - 1) - target, target)
        local.append(jnp.sum(jnp.where(rank == target, column[...], 0.0), axis=0, keepdims=True) * sign1)
    for h in range(2):
        list1[0, h:h + 1, :] = local[h]
    merged = gathered[...]
    total = merged[0:ENT] + merged[ENT:2 * ENT] + merged[2 * ENT:3 * ENT]
    for b in range(SIDE):
        cand1[b] = total[:, b * LANES:(b + 1) * LANES]

    pl.semaphore_wait(barrier, SIDE - 1 + half - 1)

    def to(src, dst, ssem, rsem, device):
        return pltpu.make_async_remote_copy(
            src_ref=src, dst_ref=dst, send_sem=ssem, recv_sem=rsem,
            device_id={"scen": device}, device_id_type=MESH,
        )

    first = [to(list1.at[0], got1.at[x], send1.at[o], recv1.at[x], o * half + yc) for o in across]
    cfirst = [to(cand1.at[o], cgot1.at[x], csend1.at[o], crecv1.at[x], o * half + yc) for o in across]
    for copy in first:
        copy.start()
    for copy in cfirst:
        copy.start()
    got1[x] = list1[0]
    cgot1[x] = cand1[x]

    def landed(dst, sem):
        pltpu.make_async_copy(dst, dst, sem).wait()

    for o in across:
        landed(got1.at[o], recv1.at[o])
    slot = iota((1, LANES), 1)
    all1 = got1[...]
    lists = jnp.concatenate([lists_down(all1[:, h, :]) for h in range(2)], axis=0)
    rising2 = yc >= half // 2
    lists = merge(lists, sign_of((slot & 4) != 0), 4, sign_of((slot & 2) != 0))
    lists = merge(lists, sign_of((slot & 2) != 0), 2, sign_of((slot & 1) != 0))
    lists = merge(lists, sign_of((slot & 1) != 0), 1, sign_of(rising2))
    for h in range(2):
        list2[0, h:h + 1, :] = along_lanes(lists[h * LANES:(h + 1) * LANES])
    second = [to(list2.at[0], got2.at[yc], send2.at[o], recv2.at[yc], x * half + o) for o in along]
    for copy in second:
        copy.start()
    got2[yc] = list2[0]

    for o in across:
        landed(cgot1.at[o], crecv1.at[o])
    cand2[0] = jnp.sum(cgot1[...], axis=0)
    csecond = [to(cand2.at[0], cgot2.at[yc], csend2.at[o], crecv2.at[yc], x * half + o) for o in along]
    for copy in csecond:
        copy.start()
    cgot2[yc] = cand2[0]

    for o in along:
        landed(got2.at[o], recv2.at[o])
    all2 = got2[...]
    lists = jnp.concatenate([lists_down(all2[:, h, :]) for h in range(2)], axis=0)
    lists = merge(lists, sign_of((slot & 8) != 0), 8, sign_of((slot & 4) != 0))
    lists = merge(lists, sign_of((slot & 4) != 0), 4, sign_of((slot & 2) != 0))
    lists = merge(lists, sign_of((slot & 2) != 0), 2, sign_of((slot & 1) != 0))
    lists = merge(lists, sign_of((slot & 1) != 0), 1, F32(1.0))
    for h in range(2):
        tail_out[h:h + 1, :] = along_lanes(lists[h * LANES:(h + 1) * LANES])

    for o in along:
        landed(cgot2.at[o], crecv2.at[o])
    summed = jnp.sum(cgot2[...], axis=0)
    flipped[...] = jnp.concatenate([summed] * (LANES // ENT), axis=0).T
    cand_out[...] = flipped[pl.ds(pl.multiple_of(yc * SUB, SUB), SUB), 0:ENT]

    for copy in first + cfirst + second + csecond:
        copy.wait_send()


def body(shocks, factor_sens, notional, moneyness, desk_entity, scenario_counts, candidate_ids):
    slots, factors = shocks.shape
    instruments = factor_sens.shape[1]
    half = SIDE * CORES
    any_space = pl.BlockSpec(memory_space=pl.ANY)
    vmem = pl.BlockSpec(memory_space=pltpu.VMEM)
    dma = pltpu.SemaphoreType.DMA
    tail, cand = pl.pallas_call(
        kernel,
        out_shape=(
            jax.ShapeDtypeStruct((2, LANES), F32),
            jax.ShapeDtypeStruct((SUB, ENT), F32),
        ),
        in_specs=[any_space] * 7,
        out_specs=(vmem, vmem),
        scratch_shapes=[
            pltpu.VMEM((slots, factors), BF16),
            pltpu.VMEM((factors, instruments), BF16),
            pltpu.VMEM((SUB, LANES), F32),
            pltpu.VMEM((SUB, LANES), F32),
            pltpu.VMEM((1, K), jnp.int32),
            pltpu.SMEM((1,), jnp.int32),
            pltpu.VMEM((SUB, LANES), jnp.int32),
            pltpu.VMEM((TILE, TILE), BF16),
            pltpu.VMEM((slots, LANES), F32),
            pltpu.VMEM((slots // LANES, SUB, LANES), F32),
            pltpu.VMEM((3 * ENT, SIDE * LANES), F32),
            pltpu.VMEM((1, 2, LANES), F32),
            pltpu.VMEM((1, 2, LANES), F32),
            pltpu.VMEM((SIDE, 2, LANES), F32),
            pltpu.VMEM((half, 2, LANES), F32),
            pltpu.VMEM((SIDE, ENT, LANES), F32),
            pltpu.VMEM((1, ENT, LANES), F32),
            pltpu.VMEM((SIDE, ENT, LANES), F32),
            pltpu.VMEM((half, ENT, LANES), F32),
            pltpu.VMEM((LANES, LANES), F32),
            dma((slots // TILE + instruments // TILE,)),
            dma((5,)),
            dma((SIDE,)), dma((SIDE,)), dma((half,)), dma((half,)),
            dma((SIDE,)), dma((SIDE,)), dma((half,)), dma((half,)),
        ],
        compiler_params=pltpu.CompilerParams(
            collective_id=0, has_side_effects=True, vmem_limit_bytes=48 * 1024 * 1024
        ),
        name="tail_search",
    )(
        shocks,
        factor_sens,
        notional.reshape(SUB, LANES),
        moneyness.reshape(SUB, LANES),
        desk_entity.reshape(1, K),
        scenario_counts,
        candidate_ids.reshape(SUB, LANES),
    )
    return tail.reshape(TOPK), cand


def solution(mesh):
    both = ("grp", "scen")
    return jax.shard_map(
        body,
        mesh=mesh,
        in_specs=(P(both, None), P(), P(), P(), P(), P(both), P("grp")),
        out_specs=(P("grp"), P(both, None)),
        check_vma=False,
    )
```

time: 102 us -> 45 us (0.44)
  the two profiles are of different devices: /device:TPU:513 before, /device:TPU:515 now
where the time goes in v1:
time: 45 us; the launch traced here: 44.5 us
  Pallas kernels  37.2 us (83%)
  local copies, waits for them, and re-layouts  6.05 us (13%)
  between operations  1.3 us (3%)
    pallas_call x1, Pallas kernels, body(): pl.pallas_call(kernel, out_shape=(jax.ShapeDtypeStruct((2, LANES), F32),...  37.2 us
    unnamed x12, local copies, waits for them, and re-layouts  6.05 us

profile of v1, /device:TPU:515, one launch (start us, length us, event | category | flops | bytes accessed | tf_op | source)
XLA Modules:
  0.0 44.5 jit_solution(7036168277360039047)
XLA Ops:
  1.3 0.0 copy-start
  1.3 2.2 %copy-done = bf16[1024,2048]{1,0:T(8,128)(2,1)S(1)} copy-done((bf16[1024,2048]{1,0:T(8,128)(2,1)S(1)}, bf16[1024,2048]{1,0:T(8,128)(2,1)}, u32[]{:S(2)}) %copy-start) | copy-done | bytes 4194328
  3.5 0.0 copy-start.1
  3.5 0.7 %copy-done.1 = f32[1024]{0:T(1024)S(1)} copy-done((f32[1024]{0:T(1024)S(1)}, f32[1024]{0:T(1024)}, u32[]{:S(2)}) %copy-start.1) | copy-done | bytes 4120
  4.2 0.0 copy-start.2
  4.2 0.7 %copy-done.2 = f32[1024]{0:T(1024)S(1)} copy-done((f32[1024]{0:T(1024)S(1)}, f32[1024]{0:T(1024)}, u32[]{:S(2)}) %copy-start.2) | copy-done | bytes 4120
  4.8 0.0 copy-start.3
  4.8 0.7 %copy-done.3 = s32[1024]{0:T(1024)S(1)} copy-done((s32[1024]{0:T(1024)S(1)}, s32[1024]{0:T(1024)}, u32[]{:S(2)}) %copy-start.3) | copy-done | bytes 4120
  5.5 0.0 copy-start.4
  5.5 0.7 %copy-done.4 = s32[64]{0:T(128)S(1)} copy-done((s32[64]{0:T(128)S(1)}, s32[64]{0:T(128)}, u32[]{:S(2)}) %copy-start.4) | copy-done | bytes 280
  6.2 37.2 %tail_search.1 = (f32[2,128]{1,0:T(2,128)S(1)}, f32[8,8]{1,0:T(8,128)S(1)}) custom-call(bf16[1024,2048]{1,0:T(8,128)(2,1)S(1)} %copy-done, bf16[2048,1024]{1,0:T(8,128)(2,1)} %sens.1, f32[8,128]{1,0:T(8,128)S(1)} %bitcast.5, f32[8,128]{1,0:T(8,128)S(1)} %bitcast.6, s32[1,64]{1,0:T(1,128)S(1)} %bitcast.9, s32[1]{0:T(128)S(6)} %copy.11.counts, ...), custom_call_target="tpu_custom_call" | custom-call | tf_op jit(solution)/shard_map/tail_search/pallas_call | solution.py:293
  43.4 0.6 %copy.12 = f32[256]{0:T(256)} copy(f32[256]{0:T(256)S(1)} %bitcast.8) | data formatting | bytes 2048
  43.9 0.6 %copy.13 = f32[8,8]{1,0:T(8,128)} copy(f32[8,8]{1,0:T(8,128)S(1)} %get-tuple-element.9) | data formatting | bytes 512
Async XLA Ops:
  1.3 2.2 %copy-start = (bf16[1024,2048]{1,0:T(8,128)(2,1)S(1)}, bf16[1024,2048]{1,0:T(8,128)(2,1)}, u32[]{:S(2)}) copy-start(bf16[1024,2048]{1,0:T(8,128)(2,1)} %shocks.1) | copy-start | bytes 12582916
  3.5 0.7 %copy-start.1 = (f32[1024]{0:T(1024)S(1)}, f32[1024]{0:T(1024)}, u32[]{:S(2)}) copy-start(f32[1024]{0:T(1024)} %param.9) | copy-start | bytes 12292
  4.2 0.7 %copy-start.2 = (f32[1024]{0:T(1024)S(1)}, f32[1024]{0:T(1024)}, u32[]{:S(2)}) copy-start(f32[1024]{0:T(1024)} %param.10) | copy-start | bytes 12292
  4.8 0.7 %copy-start.3 = (s32[1024]{0:T(1024)S(1)}, s32[1024]{0:T(1024)}, u32[]{:S(2)}) copy-start(s32[1024]{0:T(1024)} %param.13) | copy-start | bytes 12292
  5.5 0.7 %copy-start.4 = (s32[64]{0:T(128)S(1)}, s32[64]{0:T(128)}, u32[]{:S(2)}) copy-start(s32[64]{0:T(128)} %param.11) | copy-start | bytes 772

commit v2 on v1

--- a/solution.py
+++ b/solution.py
@@ -16,6 +16,10 @@
 LANES = 128
 SUB = 8
 TILE = 256
+STRIP = 32
+PIECES = 3
+FAR_SIDE = (4, 3, 5, 2, 6, 1, 7)
+FAR_HALF = (8, 9, 7, 6, 10, 5, 11, 4, 12, 3, 13, 2, 14, 1, 15)
 FLOOR = -1e30
 MESH = pl.DeviceIdType.MESH
 F32 = jnp.float32
@@ -78,26 +82,38 @@
 def kernel(
     shocks, sens, notional, moneyness, desk_entity, counts, ids,
     tail_out, cand_out,
-    sh, fs, nv, mv, dv, cv, iv, indicator, column, spread, gathered,
+    sh, fs, nv, mv, dv, cv, iv, value, base_soft, terms, indicator, column, spread, seen, gathered,
     list1, list2, got1, got2, cand1, cand2, cgot1, cgot2, flipped,
     load_sem, small_sem, send1, recv1, send2, recv2, csend1, crecv1, csend2, crecv2,
 ):
-    slots = sh.shape[0]
+    slots, factors = sh.shape
     turns = slots // TILE
-    chunks = sens.shape[1] // TILE
+    wide = sens.shape[1] // 2
+    deep = factors // 2
     me = lax.axis_index("scen")
     x, yc = me // (SIDE * CORES), me % (SIDE * CORES)
     half = SIDE * CORES
-    across = [lax.rem(x + d, SIDE) for d in range(1, SIDE)]
-    along = [lax.rem(yc + d, half) for d in range(1, half)]
-
-    def load_rows(r):
-        rows = pl.ds(r * TILE, TILE)
-        return pltpu.make_async_copy(shocks.at[rows], sh.at[rows], load_sem.at[r])
-
-    def load_columns(c):
-        cols = pl.ds(c * TILE, TILE)
-        return pltpu.make_async_copy(sens.at[:, cols], fs.at[:, cols], load_sem.at[turns + c])
+    across = [lax.rem(x + d, SIDE) for d in FAR_SIDE]
+    along = [lax.rem(yc + d, half) for d in FAR_HALF]
+
+    def copy_in(src, dst, n):
+        return pltpu.make_async_copy(src, dst, load_sem.at[n])
+
+    def part(ref, r0, rn, c0, cn):
+        return ref.at[pl.ds(r0, rn), pl.ds(c0, cn)]
+
+    def load(n, r=None):
+        if n == "rows":
+            rows = pl.ds(r * TILE, TILE)
+            return copy_in(shocks.at[rows], sh.at[rows], 4 + r)
+        if n == "right":
+            return copy_in(part(sens, 0, factors, wide, wide), part(fs, 0, factors, wide, wide), 4)
+        k = n % 2
+        if n < 2:
+            where = (0, TILE, k * deep, deep)
+            return copy_in(part(shocks, *where), part(sh, *where), n)
+        where = (k * deep, deep, 0, wide)
+        return copy_in(part(sens, *where), part(fs, *where), n)
 
     small = [
         pltpu.make_async_copy(src, dst, small_sem.at[n])
@@ -105,14 +121,13 @@
             [(moneyness, mv), (notional, nv), (desk_entity, dv), (counts, cv), (ids, iv)]
         )
     ]
-    load_rows(0).start()
-    load_columns(0).start()
+    for n in (0, 2, 1, 3):
+        load(n).start()
     for copy in small:
         copy.start()
-    for c in range(1, chunks):
-        load_columns(c).start()
     for r in range(1, turns):
-        load_rows(r).start()
+        load("rows", r).start()
+    load("right").start()
 
     barrier = pltpu.get_barrier_semaphore()
     for other in across:
@@ -132,39 +147,43 @@
     member = jnp.where(row < ENT, row, jnp.where(row >= LANES, -2, -3))
     hit = (entity == member) | ((member == -2) & (iota((TILE, LANES), 1) < K))
     owner = jnp.where(hit, -1.0, 0.0).astype(BF16)
-    indicator[...] = lax.dot_general(
+    owner = lax.dot_general(
         place, owner, (((1,), (1,)), ((), ())), preferred_element_type=F32
     ).astype(BF16)
+    for p in range(PIECES):
+        indicator[p * TILE:(p + 1) * TILE, :] = owner
+    money = mv[...]
+    base_soft[...] = jnp.maximum(money, 0.0) + jnp.log(1.0 + jnp.exp(-jnp.abs(money)))
     gathered[...] = jnp.zeros(gathered.shape, F32)
     base = me * slots
     count = cv[0]
 
-    def turn(r, first):
-        load_rows(r).wait()
-        rows = sh[pl.ds(r * TILE, TILE), :]
-        sums = []
-        for c in range(chunks):
-            if first:
-                load_columns(c).wait()
-            value = jnp.dot(rows, fs[:, c * TILE:(c + 1) * TILE], preferred_element_type=F32)
-            halves = []
-            for h in range(2):
-                b = 2 * c + h
-                m = mv[b:b + 1, :]
-                start = jnp.maximum(m, 0.0) + jnp.log(1.0 + jnp.exp(-jnp.abs(m)))
-                v = value[:, h * LANES:(h + 1) * LANES] + m
+    def price(r, c):
+        for s in range(0, TILE, STRIP):
+            quads = []
+            for h in range(4):
+                b = 4 * c + h
+                v = value[s:s + STRIP, h * LANES:(h + 1) * LANES] + mv[b:b + 1, :]
                 soft = jnp.maximum(v, 0.0) + jnp.log(1.0 + jnp.exp(-jnp.abs(v)))
-                halves.append(nv[b:b + 1, :] * (soft - start))
-            sums.append(pair_sum(halves[0], halves[1], 8))
-        parts = jnp.concatenate(
-            [pair_sum(sums[0], sums[1], 4), pair_sum(sums[2], sums[3], 4)], axis=1
+                quads.append(nv[b:b + 1, :] * (soft - base_soft[b:b + 1, :]))
+            sums = pair_sum(
+                pair_sum(quads[0], quads[1], 8), pair_sum(quads[2], quads[3], 8), 4
+            )
+            for p, term in enumerate(pieces(sums, PIECES)):
+                at = p * TILE + c * LANES
+                terms[pl.ds(r * TILE + s, STRIP), at:at + LANES] = term.astype(BF16)
+
+    def multiply(r, c):
+        value[...] = jnp.dot(
+            sh[pl.ds(r * TILE, TILE), :], fs[:, c * wide:(c + 1) * wide], preferred_element_type=F32
         )
-        total = jnp.zeros((TILE, TILE), F32)
-        for part in pieces(parts, 3):
-            total += jnp.dot(part.astype(BF16), indicator[...], preferred_element_type=F32)
+
+    def finish(r):
+        rows = slice(r * TILE, (r + 1) * TILE)
+        total = jnp.dot(terms[rows, :], indicator[...], preferred_element_type=F32)
         here = r * TILE + iota((TILE, LANES), 0)
         loss = jnp.where(here < count, total[:, LANES:], FLOOR)
-        column[pl.ds(r * TILE, TILE), :] = loss
+        column[rows, :] = loss
         for h in range(2):
             spread[2 * r + h] = loss[h * LANES:(h + 1) * LANES].T[0:SUB]
         by_entity = total[:, :LANES].T[0:ENT]
@@ -178,19 +197,14 @@
         )
         gathered[...] += jnp.dot(left, wanted, preferred_element_type=F32)
 
-    turn(0, True)
-
-    @pl.loop(1, turns)
-    def _(r):
-        turn(r, False)
-
-    blocks = slots // LANES
-    groups = slots // SUB
-    level = []
-    for i in range(blocks):
-        mine = column[i * LANES:(i + 1) * LANES, :].reshape(LANES // SUB, SUB, LANES)
-        seen = jnp.zeros(mine.shape, F32)
-        for b in range(blocks):
+    def compare(i, bs, fresh):
+        rows = slice(i * LANES, (i + 1) * LANES)
+        mine = column[rows, :].reshape(LANES // SUB, SUB, LANES)
+        if fresh:
+            before = jnp.zeros(mine.shape, F32)
+        else:
+            before = seen[rows, :].reshape(mine.shape)
+        for b in bs:
             theirs = spread[b][None]
             if b < i:
                 ahead = theirs >= mine
@@ -199,20 +213,58 @@
             else:
                 own = iota(mine.shape, 0) * SUB + iota(mine.shape, 1)
                 ahead = (theirs > mine) | ((theirs == mine) & (iota(mine.shape, 2) < own))
-            seen = jnp.where(ahead, seen + 1.0, seen)
-        level.append(seen.reshape(LANES, LANES))
-    seen = jnp.concatenate(level, axis=0).astype(BF16)
-    rank = jnp.dot(seen, jnp.ones((LANES, LANES), BF16), preferred_element_type=F32)
+            before = jnp.where(ahead, before + 1.0, before)
+        seen[rows, :] = before.reshape(LANES, LANES)
+
+    def rank(r):
+        for i in range(2 * r):
+            compare(i, (2 * r, 2 * r + 1), False)
+        for i in (2 * r, 2 * r + 1):
+            compare(i, range(2 * r + 2), True)
+
+    load(0).wait()
+    load(2).wait()
+    value[...] = jnp.dot(sh[0:TILE, 0:deep], fs[0:deep, 0:wide], preferred_element_type=F32)
+    load(1).wait()
+    load(3).wait()
+    value[...] += jnp.dot(sh[0:TILE, deep:], fs[deep:, 0:wide], preferred_element_type=F32)
+
+    @pl.loop(1, turns)
+    def _(r):
+        load("rows", r).wait()
+        price(r - 1, 0)
+        multiply(r, 0)
+
+    load("right").wait()
+    price(turns - 1, 0)
+    multiply(0, 1)
+    for r in range(turns):
+        if r > 1:
+            rank(r - 2)
+        if r > 0:
+            finish(r - 1)
+        price(r, 1)
+        if r < turns - 1:
+            multiply(r + 1, 1)
+    rank(turns - 2)
+    finish(turns - 1)
+    rank(turns - 1)
 
     rising1 = x >= SIDE // 2
     sign1 = sign_of(rising1)
-    local = []
+    targets = []
     for h in range(2):
         target = iota((1, LANES), 1).astype(F32) + float(h * LANES)
-        target = jnp.where(rising1, float(TOPK - 1) - target, target)
-        local.append(jnp.sum(jnp.where(rank == target, column[...], 0.0), axis=0, keepdims=True) * sign1)
+        targets.append(jnp.where(rising1, float(TOPK - 1) - target, target))
+    local = [jnp.zeros((SUB, LANES), F32) for _ in range(2)]
+    for i in range(slots // LANES):
+        rows = slice(i * LANES, (i + 1) * LANES)
+        place = jnp.sum(seen[rows, :], axis=1, keepdims=True)
+        for h in range(2):
+            chosen = jnp.where(place == targets[h], column[rows, :], 0.0)
+            local[h] += jnp.sum(chosen.reshape(LANES // SUB, SUB, LANES), axis=0)
     for h in range(2):
-        list1[0, h:h + 1, :] = local[h]
+        list1[0, h:h + 1, :] = jnp.sum(local[h], axis=0, keepdims=True) * sign1
     merged = gathered[...]
     total = merged[0:ENT] + merged[ENT:2 * ENT] + merged[2 * ENT:3 * ENT]
     for b in range(SIDE):
@@ -287,7 +339,7 @@
     slots, factors = shocks.shape
     instruments = factor_sens.shape[1]
     half = SIDE * CORES
-    any_space = pl.BlockSpec(memory_space=pl.ANY)
+    hbm = pl.BlockSpec(memory_space=pltpu.HBM)
     vmem = pl.BlockSpec(memory_space=pltpu.VMEM)
     dma = pltpu.SemaphoreType.DMA
     tail, cand = pl.pallas_call(
@@ -296,7 +348,7 @@
             jax.ShapeDtypeStruct((2, LANES), F32),
             jax.ShapeDtypeStruct((SUB, ENT), F32),
         ),
-        in_specs=[any_space] * 7,
+        in_specs=[hbm] * 7,
         out_specs=(vmem, vmem),
         scratch_shapes=[
             pltpu.VMEM((slots, factors), BF16),
@@ -306,9 +358,13 @@
             pltpu.VMEM((1, K), jnp.int32),
             pltpu.SMEM((1,), jnp.int32),
             pltpu.VMEM((SUB, LANES), jnp.int32),
-            pltpu.VMEM((TILE, TILE), BF16),
+            pltpu.VMEM((TILE, instruments // 2), F32),
+            pltpu.VMEM((SUB, LANES), F32),
+            pltpu.VMEM((slots, PIECES * TILE), BF16),
+            pltpu.VMEM((PIECES * TILE, TILE), BF16),
             pltpu.VMEM((slots, LANES), F32),
             pltpu.VMEM((slots // LANES, SUB, LANES), F32),
+            pltpu.VMEM((slots, LANES), F32),
             pltpu.VMEM((3 * ENT, SIDE * LANES), F32),
             pltpu.VMEM((1, 2, LANES), F32),
             pltpu.VMEM((1, 2, LANES), F32),
@@ -319,13 +375,13 @@
             pltpu.VMEM((SIDE, ENT, LANES), F32),
             pltpu.VMEM((half, ENT, LANES), F32),
             pltpu.VMEM((LANES, LANES), F32),
-            dma((slots // TILE + instruments // TILE,)),
+            dma((4 + slots // TILE,)),
             dma((5,)),
             dma((SIDE,)), dma((SIDE,)), dma((half,)), dma((half,)),
             dma((SIDE,)), dma((SIDE,)), dma((half,)), dma((half,)),
         ],
         compiler_params=pltpu.CompilerParams(
-            collective_id=0, has_side_effects=True, vmem_limit_bytes=48 * 1024 * 1024
+            collective_id=0, has_side_effects=True, vmem_limit_bytes=67043328
         ),
         name="tail_search",
     )(

time: 45 us -> 40.4 us (0.90)
  local copies, waits for them, and re-layouts: 6.05 us -> 2.48 us
  Pallas kernels: 37.2 us -> 36.4 us
    unnamed x12 -> x2, local copies, waits for them, and re-layouts: 6.05 us -> 2.48 us
    pallas_call x1, Pallas kernels: 37.2 us -> 36.4 us  [body(): pl.pallas_call(kernel, out_shape=(jax.ShapeDtypeStruct((2, LANES), F32),...]
where the time goes in v2:
time: 40.4 us; the launch traced here: 40.2 us
  Pallas kernels  36.4 us (90%)
  local copies, waits for them, and re-layouts  2.48 us (6%)
  between operations  1.29 us (3%)
    pallas_call x1, Pallas kernels, body(): pl.pallas_call(kernel, out_shape=(jax.ShapeDtypeStruct((2, LANES), F32),...  36.4 us
    unnamed x2, local copies, waits for them, and re-layouts  2.48 us

profile of v2, /device:TPU:515, one launch (start us, length us, event | category | flops | bytes accessed | tf_op | source)
XLA Modules:
  0.0 40.2 jit_solution(3793683910568875739)
XLA Ops:
  1.3 36.4 %tail_search.1 = (f32[2,128]{1,0:T(2,128)}, f32[8,8]{1,0:T(8,128)}) custom-call(bf16[1024,2048]{1,0:T(8,128)(2,1)} %shocks.1, bf16[2048,1024]{1,0:T(8,128)(2,1)} %sens.1, f32[8,128]{1,0:T(8,128)} %bitcast.5, f32[8,128]{1,0:T(8,128)} %bitcast.6, s32[1,64]{1,0:T(1,128)} %bitcast.9, s32[1]{0:T(128)S(6)} %copy.11.counts, s32[8,128]{1,0:T(8,128)} %bitcast.7), custom_call_target="tpu_custom_call" | custom-call | tf_op jit(solution)/shard_map/tail_search/pallas_call | solution.py:345
  37.7 1.2 %copy.12 = f32[256]{0:T(256)} copy(f32[256]{0:T(256)} %bitcast.8) | data formatting | bytes 2048
  38.9 1.3 %copy.13 = f32[8,8]{1,0:T(8,128)} copy(f32[8,8]{1,0:T(8,128)} %get-tuple-element.9) | data formatting | bytes 512

commit v3 on v2

--- a/solution.py
+++ b/solution.py
@@ -80,9 +80,9 @@
 
 
 def kernel(
-    shocks, sens, notional, moneyness, desk_entity, counts, ids,
+    cv, shocks, sens, notional, moneyness, desk_entity, ids,
     tail_out, cand_out,
-    sh, fs, nv, mv, dv, cv, iv, value, base_soft, terms, indicator, column, spread, seen, gathered,
+    sh, fs, nv, mv, dv, iv, value, base_soft, terms, indicator, column, spread, seen, gathered,
     list1, list2, got1, got2, cand1, cand2, cgot1, cgot2, flipped,
     load_sem, small_sem, send1, recv1, send2, recv2, csend1, crecv1, csend2, crecv2,
 ):
@@ -118,7 +118,7 @@
     small = [
         pltpu.make_async_copy(src, dst, small_sem.at[n])
         for n, (src, dst) in enumerate(
-            [(moneyness, mv), (notional, nv), (desk_entity, dv), (counts, cv), (ids, iv)]
+            [(moneyness, mv), (notional, nv), (desk_entity, dv), (ids, iv)]
         )
     ]
     for n in (0, 2, 1, 3):
@@ -138,10 +138,9 @@
     for copy in small:
         copy.wait()
 
-    lane = iota((TILE, LANES), 0)
-    within = lane % LANES
-    desk = 8 * (4 * (lane // LANES) + 2 * ((within // 4) % 2) + (within // 8) % 2) + within // 16
-    place = jnp.where(desk == iota((TILE, LANES), 1), 1.0, 0.0).astype(BF16)
+    lane = iota((LANES, LANES), 0)
+    desk = 8 * (4 * ((lane // 2) % 2) + 2 * ((lane // 4) % 2) + (lane // 8) % 2) + lane // 16
+    place = jnp.where(desk == iota((LANES, LANES), 1), 1.0, 0.0).astype(BF16)
     entity = jnp.concatenate([dv[...], jnp.full((1, LANES - K), -1, jnp.int32)], axis=1)
     row = iota((TILE, LANES), 0)
     member = jnp.where(row < ENT, row, jnp.where(row >= LANES, -2, -3))
@@ -151,7 +150,7 @@
         place, owner, (((1,), (1,)), ((), ())), preferred_element_type=F32
     ).astype(BF16)
     for p in range(PIECES):
-        indicator[p * TILE:(p + 1) * TILE, :] = owner
+        indicator[p * LANES:(p + 1) * LANES, :] = owner
     money = mv[...]
     base_soft[...] = jnp.maximum(money, 0.0) + jnp.log(1.0 + jnp.exp(-jnp.abs(money)))
     gathered[...] = jnp.zeros(gathered.shape, F32)
@@ -169,9 +168,13 @@
             sums = pair_sum(
                 pair_sum(quads[0], quads[1], 8), pair_sum(quads[2], quads[3], 8), 4
             )
-            for p, term in enumerate(pieces(sums, PIECES)):
-                at = p * TILE + c * LANES
-                terms[pl.ds(r * TILE + s, STRIP), at:at + LANES] = term.astype(BF16)
+            rows = pl.ds(r * TILE + s, STRIP)
+            if c == 0:
+                column[rows, :] = sums
+            else:
+                sums = pair_sum(column[rows, :], sums, 2)
+                for p, term in enumerate(pieces(sums, PIECES)):
+                    terms[rows, p * LANES:(p + 1) * LANES] = term.astype(BF16)
 
     def multiply(r, c):
         value[...] = jnp.dot(
@@ -180,7 +183,16 @@
 
     def finish(r):
         rows = slice(r * TILE, (r + 1) * TILE)
-        total = jnp.dot(terms[rows, :], indicator[...], preferred_element_type=F32)
+        total = jnp.concatenate(
+            [
+                jnp.dot(
+                    terms[r * TILE + h * LANES:r * TILE + (h + 1) * LANES, :], indicator[...],
+                    preferred_element_type=F32,
+                )
+                for h in range(2)
+            ],
+            axis=0,
+        )
         here = r * TILE + iota((TILE, LANES), 0)
         loss = jnp.where(here < count, total[:, LANES:], FLOOR)
         column[rows, :] = loss
@@ -278,8 +290,8 @@
             device_id={"scen": device}, device_id_type=MESH,
         )
 
-    first = [to(list1.at[0], got1.at[x], send1.at[o], recv1.at[x], o * half + yc) for o in across]
-    cfirst = [to(cand1.at[o], cgot1.at[x], csend1.at[o], crecv1.at[x], o * half + yc) for o in across]
+    first = [to(list1.at[0], got1.at[x], send1, recv1, o * half + yc) for o in across]
+    cfirst = [to(cand1.at[o], cgot1.at[x], csend1, crecv1, o * half + yc) for o in across]
     for copy in first:
         copy.start()
     for copy in cfirst:
@@ -287,11 +299,11 @@
     got1[x] = list1[0]
     cgot1[x] = cand1[x]
 
-    def landed(dst, sem):
-        pltpu.make_async_copy(dst, dst, sem).wait()
-
-    for o in across:
-        landed(got1.at[o], recv1.at[o])
+    def settle(slots_of, others, sem):
+        every = slots_of.at[pl.ds(0, others)]
+        pltpu.make_async_copy(every, every, sem).wait()
+
+    settle(got1, SIDE - 1, recv1)
     slot = iota((1, LANES), 1)
     all1 = got1[...]
     lists = jnp.concatenate([lists_down(all1[:, h, :]) for h in range(2)], axis=0)
@@ -301,21 +313,19 @@
     lists = merge(lists, sign_of((slot & 1) != 0), 1, sign_of(rising2))
     for h in range(2):
         list2[0, h:h + 1, :] = along_lanes(lists[h * LANES:(h + 1) * LANES])
-    second = [to(list2.at[0], got2.at[yc], send2.at[o], recv2.at[yc], x * half + o) for o in along]
+    second = [to(list2.at[0], got2.at[yc], send2, recv2, x * half + o) for o in along]
     for copy in second:
         copy.start()
     got2[yc] = list2[0]
 
-    for o in across:
-        landed(cgot1.at[o], crecv1.at[o])
+    settle(cgot1, SIDE - 1, crecv1)
     cand2[0] = jnp.sum(cgot1[...], axis=0)
-    csecond = [to(cand2.at[0], cgot2.at[yc], csend2.at[o], crecv2.at[yc], x * half + o) for o in along]
+    csecond = [to(cand2.at[0], cgot2.at[yc], csend2, crecv2, x * half + o) for o in along]
     for copy in csecond:
         copy.start()
     cgot2[yc] = cand2[0]
 
-    for o in along:
-        landed(got2.at[o], recv2.at[o])
+    settle(got2, half - 1, recv2)
     all2 = got2[...]
     lists = jnp.concatenate([lists_down(all2[:, h, :]) for h in range(2)], axis=0)
     lists = merge(lists, sign_of((slot & 8) != 0), 8, sign_of((slot & 4) != 0))
@@ -325,14 +335,15 @@
     for h in range(2):
         tail_out[h:h + 1, :] = along_lanes(lists[h * LANES:(h + 1) * LANES])
 
-    for o in along:
-        landed(cgot2.at[o], crecv2.at[o])
+    settle(cgot2, half - 1, crecv2)
     summed = jnp.sum(cgot2[...], axis=0)
     flipped[...] = jnp.concatenate([summed] * (LANES // ENT), axis=0).T
     cand_out[...] = flipped[pl.ds(pl.multiple_of(yc * SUB, SUB), SUB), 0:ENT]
 
-    for copy in first + cfirst + second + csecond:
-        copy.wait_send()
+    settle(got1, SIDE - 1, send1)
+    settle(cgot1, SIDE - 1, csend1)
+    settle(got2, half - 1, send2)
+    settle(cgot2, half - 1, csend2)
 
 
 def body(shocks, factor_sens, notional, moneyness, desk_entity, scenario_counts, candidate_ids):
@@ -345,10 +356,10 @@
     tail, cand = pl.pallas_call(
         kernel,
         out_shape=(
-            jax.ShapeDtypeStruct((2, LANES), F32),
-            jax.ShapeDtypeStruct((SUB, ENT), F32),
+            pltpu.VMEM((2, LANES), F32),
+            pltpu.VMEM((SUB, ENT), F32),
         ),
-        in_specs=[hbm] * 7,
+        in_specs=[pl.BlockSpec(memory_space=pltpu.SMEM)] + [hbm] * 6,
         out_specs=(vmem, vmem),
         scratch_shapes=[
             pltpu.VMEM((slots, factors), BF16),
@@ -356,12 +367,11 @@
             pltpu.VMEM((SUB, LANES), F32),
             pltpu.VMEM((SUB, LANES), F32),
             pltpu.VMEM((1, K), jnp.int32),
-            pltpu.SMEM((1,), jnp.int32),
             pltpu.VMEM((SUB, LANES), jnp.int32),
             pltpu.VMEM((TILE, instruments // 2), F32),
             pltpu.VMEM((SUB, LANES), F32),
-            pltpu.VMEM((slots, PIECES * TILE), BF16),
-            pltpu.VMEM((PIECES * TILE, TILE), BF16),
+            pltpu.VMEM((slots, PIECES * LANES), BF16),
+            pltpu.VMEM((PIECES * LANES, TILE), BF16),
             pltpu.VMEM((slots, LANES), F32),
             pltpu.VMEM((slots // LANES, SUB, LANES), F32),
             pltpu.VMEM((slots, LANES), F32),
@@ -376,22 +386,26 @@
             pltpu.VMEM((half, ENT, LANES), F32),
             pltpu.VMEM((LANES, LANES), F32),
             dma((4 + slots // TILE,)),
-            dma((5,)),
-            dma((SIDE,)), dma((SIDE,)), dma((half,)), dma((half,)),
-            dma((SIDE,)), dma((SIDE,)), dma((half,)), dma((half,)),
+            dma((4,)),
+            dma, dma, dma, dma, dma, dma, dma, dma,
         ],
         compiler_params=pltpu.CompilerParams(
-            collective_id=0, has_side_effects=True, vmem_limit_bytes=67043328
+            collective_id=0, has_side_effects=True, vmem_limit_bytes=48 * 1024 * 1024
         ),
         name="tail_search",
     )(
-        shocks,
-        factor_sens,
-        notional.reshape(SUB, LANES),
-        moneyness.reshape(SUB, LANES),
-        desk_entity.reshape(1, K),
         scenario_counts,
-        candidate_ids.reshape(SUB, LANES),
+        *[
+            pltpu.with_memory_space_constraint(array, pltpu.HBM)
+            for array in (
+                shocks,
+                factor_sens,
+                notional.reshape(SUB, LANES),
+                moneyness.reshape(SUB, LANES),
+                desk_entity.reshape(1, K),
+                candidate_ids.reshape(SUB, LANES),
+            )
+        ],
     )
     return tail.reshape(TOPK), cand
 

time: 40.4 us -> 37.7 us (0.933)
  local copies, waits for them, and re-layouts: 2.48 us -> 1.16 us
  Pallas kernels: 36.4 us -> 35.1 us
    unnamed x2, local copies, waits for them, and re-layouts: 2.48 us -> 1.16 us
    pallas_call x1, Pallas kernels: 36.4 us -> 35.1 us  [body(): pl.pallas_call(kernel, out_shape=(pltpu.VMEM((2, LANES), F32), pltpu.VMEM...]
where the time goes in v3:
time: 37.7 us; the launch traced here: 37.6 us
  Pallas kernels  35.1 us (93%)
  between operations  1.29 us (3%)
  local copies, waits for them, and re-layouts  1.16 us (3%)
    pallas_call x1, Pallas kernels, body(): pl.pallas_call(kernel, out_shape=(pltpu.VMEM((2, LANES), F32), pltpu.VMEM...  35.1 us
    unnamed x2, local copies, waits for them, and re-layouts  1.16 us

profile of v3, /device:TPU:515, one launch (start us, length us, event | category | flops | bytes accessed | tf_op | source)
XLA Modules:
  0.0 37.6 jit_solution(14819118556575818186)
XLA Ops:
  1.3 35.1 %tail_search.1 = (f32[2,128]{1,0:T(2,128)S(1)}, f32[8,8]{1,0:T(8,128)S(1)}) custom-call(s32[1]{0:T(128)S(6)} %copy.13.cv, bf16[1024,2048]{1,0:T(8,128)(2,1)} %shocks.1, bf16[2048,1024]{1,0:T(8,128)(2,1)} %sens.1, f32[8,128]{1,0:T(8,128)} %bitcast.6, f32[8,128]{1,0:T(8,128)} %bitcast.7, s32[1,64]{1,0:T(1,128)} %bitcast.9, s32[8,128]{1,0:T(8,128)} %bitcast.8), custom_call_target="tpu_custom_call" | custom-call | tf_op jit(solution)/shard_map/tail_search/pallas_call | solution.py:356
  36.4 0.6 %copy.11 = f32[256]{0:T(256)} copy(f32[256]{0:T(256)S(1)} %bitcast.5) | data formatting | bytes 2048
  37.0 0.6 %copy.12 = f32[8,8]{1,0:T(8,128)} copy(f32[8,8]{1,0:T(8,128)S(1)} %get-tuple-element.7) | data formatting | bytes 512

commit v4 on v3

v4 whole, which is shorter than its diff:
```python
import functools

import jax
import jax.numpy as jnp
from jax import lax
from jax.experimental import pallas as pl
from jax.experimental.pallas import tpu as pltpu
from jax.sharding import PartitionSpec as P

K = 64
INSTR = 16
ENT = 8
TOPK = 256
SIDE = 8
CORES = 2
LANES = 128
SUB = 8
TILE = 256
STRIP = 32
PIECES = 3
FIRST = 4
FAR_SIDE = (4, 3, 5, 2, 6, 1, 7)
FAR_HALF = (8, 9, 7, 6, 10, 5, 11, 4, 12, 3, 13, 2, 14, 1, 15)
FLOOR = -1e30
MESH = pl.DeviceIdType.MESH
F32 = jnp.float32
BF16 = jnp.bfloat16


def iota(shape, dim):
    return lax.broadcasted_iota(jnp.int32, shape, dim)


def pieces(array, count):
    out = []
    for _ in range(count):
        part = array.astype(BF16).astype(F32)
        out.append(part)
        array = array - part
    return out


def pair_sum(left, right, step):
    low = (iota(left.shape, 1) & step) == 0
    up = left + pltpu.roll(left, LANES - step, 1)
    down = right + pltpu.roll(right, step, 1)
    return jnp.where(low, up, down)


def merge(stored, own, step, after):
    value = stored * own
    x = jnp.maximum(value, pltpu.roll(value, step, 1)) * after
    for stride in (128, 64, 32, 16, 8):
        y = x.reshape(TOPK // (2 * stride), 2, stride, LANES)
        a, b = y[:, 0], y[:, 1]
        x = jnp.stack([jnp.maximum(a, b), jnp.minimum(a, b)], axis=1).reshape(TOPK, LANES)
    y = x.reshape(TOPK // SUB, SUB, LANES)
    at = iota(y.shape, 1)
    for stride in (4, 2, 1):
        low = (at & stride) == 0
        if stride == 4:
            other = pltpu.roll(y, 4, 1)
        else:
            other = jnp.where(low, pltpu.roll(y, SUB - stride, 1), pltpu.roll(y, stride, 1))
        y = jnp.where(low, jnp.maximum(y, other), jnp.minimum(y, other))
    return y.reshape(TOPK, LANES)


def lists_down(rows):
    copies = LANES // rows.shape[0]
    return jnp.concatenate([rows] * copies, axis=0).T


def along_lanes(column):
    same = iota(column.shape, 0) == iota(column.shape, 1)
    return jnp.sum(jnp.where(same, column, 0.0), axis=0, keepdims=True)


def sign_of(bit):
    return jnp.where(bit, F32(-1.0), F32(1.0))


def search(
    units, cv, shocks, sens, notional, moneyness, desk_entity, ids,
    tail_out, cand_out,
    sh, fs, nv, mv, dv, iv, base_soft, terms, indicator, column, spread, seen, by_entity, split,
    list1, list2, got1, got2, cand1, cand2, cgot1, cgot2, flipped,
    load_sem, small_sem, send1, recv1, send2, recv2, csend1, crecv1, csend2, crecv2,
):
    slots, factors = sh.shape
    turns = slots // TILE
    wide = sens.shape[1] // 2
    deep = factors // FIRST
    me = lax.axis_index("scen")
    x, yc = me // (SIDE * CORES), me % (SIDE * CORES)
    half = SIDE * CORES
    across = [lax.rem(x + d, SIDE) for d in FAR_SIDE]
    along = [lax.rem(yc + d, half) for d in FAR_HALF]

    def copy_in(src, dst, n):
        return pltpu.make_async_copy(src, dst, load_sem.at[n])

    def part(ref, r0, rn, c0, cn):
        return ref.at[pl.ds(r0, rn), pl.ds(c0, cn)]

    def load(n, r=None):
        if n == "rows":
            rows = pl.ds(r * TILE, TILE)
            return copy_in(shocks.at[rows], sh.at[rows], 2 * FIRST + r)
        if n == "right":
            return copy_in(part(sens, 0, factors, wide, wide), part(fs, 0, factors, wide, wide), 2 * FIRST)
        at = n % FIRST * deep
        if n < FIRST:
            where = (0, TILE, at, deep)
            return copy_in(part(shocks, *where), part(sh, *where), n)
        where = (at, deep, 0, wide)
        return copy_in(part(sens, *where), part(fs, *where), n)

    small = [
        pltpu.make_async_copy(src, dst, small_sem.at[n])
        for n, (src, dst) in enumerate(
            [(moneyness, mv), (notional, nv), (desk_entity, dv), (ids, iv)]
        )
    ]
    for n in range(FIRST):
        load(n).start()
        load(FIRST + n).start()
    for copy in small:
        copy.start()
    for r in range(1, turns):
        load("rows", r).start()
    load("right").start()

    barrier = pltpu.get_barrier_semaphore()
    for other in across:
        pl.semaphore_signal(barrier, inc=1, device_id={"scen": other * half + yc}, device_id_type=MESH)
    for other in along:
        pl.semaphore_signal(barrier, inc=1, device_id={"scen": x * half + other}, device_id_type=MESH)

    for copy in small:
        copy.wait()

    lane = iota((LANES, LANES), 0)
    desk = 8 * (4 * ((lane // 2) % 2) + 2 * ((lane // 4) % 2) + (lane // 8) % 2) + lane // 16
    entity = jnp.concatenate([dv[...], jnp.full((1, LANES - K), -1, jnp.int32)], axis=1).astype(F32)
    entity = jnp.sum(jnp.where(desk == iota((LANES, LANES), 1), entity, 0.0), axis=1, keepdims=True)
    target = iota((LANES, TILE), 1)
    hit = (entity == target.astype(F32)) | (target >= LANES)
    owner = jnp.where(hit, -1.0, 0.0).astype(BF16)
    for p in range(PIECES):
        indicator[p * LANES:(p + 1) * LANES, :] = owner
    indicator[PIECES * LANES:, :] = jnp.zeros((LANES, TILE), BF16)
    terms[:, PIECES * LANES:] = jnp.zeros((slots, LANES), BF16)
    money = mv[...]
    base_soft[...] = jnp.maximum(money, 0.0) + jnp.log(1.0 + jnp.exp(-jnp.abs(money)))
    base = me * slots
    count = cv[0]

    free = [[0, 1], [0, 1]]
    for array in jax.tree.leaves(units):
        pltpu.matmul_pop(array)

    def push(m, tile):
        register = free[m].pop(0)
        pltpu.matmul_push_rhs(tile, register, m)
        return register

    def multiply(m, total, left, register):
        pltpu.matmul_acc_lhs(total, left, register)
        if register is not None:
            free[m].append(register)

    depth = factors // TILE
    tiles = [(c, r * TILE, TILE) for c in range(2) for r in range(turns)]
    order = [(k, t) for k in range(len(tiles)) for t in range(depth)]
    staged = []

    def stage(n):
        if n < len(order):
            k, t = order[n]
            c = tiles[k][0]
            staged.append([
                push(m, fs[t * TILE:(t + 1) * TILE, (2 * c + m) * TILE:(2 * c + m + 1) * TILE])
                for m in range(2)
            ])

    def step(n, hold):
        k, t = order[n]
        _, first, height = tiles[k]
        if not hold:
            stage(n + 1)
        registers = staged.pop(0)
        for q in range(0, height, STRIP):
            left = sh[first + q:first + q + STRIP, t * TILE:(t + 1) * TILE]
            for m in range(2):
                multiply(m, units[m]["value"][k % 2][q // STRIP], left, registers[m] if q == 0 else None)
        if hold and k == 0 and t == depth - 1:
            stage(n + 1)

    def price(k, s):
        c, first, _ = tiles[k]
        quads = []
        for m in range(2):
            found = pltpu.matmul_pop(units[m]["value"][k % 2][s // STRIP])
            for h in range(2):
                b = 4 * c + 2 * m + h
                v = found[:, h * LANES:(h + 1) * LANES] + mv[b:b + 1, :]
                soft = jnp.maximum(v, 0.0) + jnp.log(1.0 + jnp.exp(-jnp.abs(v)))
                quads.append(nv[b:b + 1, :] * (soft - base_soft[b:b + 1, :]))
        sums = pair_sum(pair_sum(quads[0], quads[1], 8), pair_sum(quads[2], quads[3], 8), 4)
        rows = slice(first + s, first + s + STRIP)
        if c == 0:
            column[rows, :] = sums
        else:
            sums = pair_sum(column[rows, :], sums, 2)
            for p, term in enumerate(pieces(sums, PIECES)):
                terms[rows, p * LANES:(p + 1) * LANES] = term.astype(BF16)

    def total_loss(r):
        for t in range(2):
            for m in range(2):
                at = r * TILE + m * LANES
                register = push(m, indicator[t * TILE:(t + 1) * TILE, :])
                multiply(m, units[m]["sums"], terms[at:at + LANES, t * TILE:(t + 1) * TILE], register)

    def spread_loss(r):
        for m in range(2):
            i = 2 * r + m
            total = pltpu.matmul_pop(units[m]["sums"])
            loss = jnp.where(i * LANES + iota((LANES, LANES), 0) < count, total[:, LANES:], FLOOR)
            column[i * LANES:(i + 1) * LANES, :] = loss
            spread[i] = loss.T[0:SUB]
            by_entity[i] = total[:, :LANES].T[0:ENT]

    def split_sums(r):
        found = pieces(jnp.concatenate([by_entity[2 * r], by_entity[2 * r + 1]], axis=1), 3)
        split[...] = jnp.concatenate(found + [jnp.zeros((ENT, TILE), F32)], axis=0).astype(BF16)

    def gather(r, t):
        here = base + r * TILE + iota((TILE, LANES), 0)
        for m in range(2):
            b = 4 * m + 2 * t
            wanted = jnp.concatenate(
                [jnp.where(iv[b + h:b + h + 1, :] == here, 1.0, 0.0).astype(BF16) for h in range(2)], axis=1
            )
            register = push(m, wanted)
            multiply(m, units[m]["gather"][t], split[...], register)

    def compare(i, b):
        mine = column[i * LANES:(i + 1) * LANES, :].reshape(LANES // SUB, SUB, LANES)
        theirs = spread[b][None]
        if i < b:
            ahead = mine >= theirs
        elif i > b:
            ahead = mine > theirs
        else:
            at = iota(mine.shape, 0) * SUB + iota(mine.shape, 1)
            ahead = (mine > theirs) | ((mine == theirs) & (at < iota(mine.shape, 2)))
        seen[b] += jnp.sum(jnp.where(ahead, 1.0, 0.0), axis=0)

    def rank(blocks):
        old = range(blocks[0])
        for b in old:
            for i in blocks:
                compare(i, b)
        for b in blocks:
            for i in (*old, *blocks):
                compare(i, b)

    def chunk(k, **work):
        @pl.when(me >= 0)
        def _():
            for t in range(depth):
                if k == 0 and t % 2 == 0:
                    load(t // 2).wait()
                    load(FIRST + t // 2).wait()
                    stage(t)
                if k == turns - 1 and t == depth - 1:
                    load("right").wait()
                step(k * depth + t, k == 0 and t % 2 == 1)
                if k > 0:
                    price(k - 1, t * STRIP)
                for piece in work.get("at%d" % t, ()):
                    piece()

    pairs = [(2 * r, 2 * r + 1) for r in range(turns)]
    seen[...] = jnp.zeros(seen.shape, F32)
    chunk(0)
    for k in range(1, turns):
        load("rows", k).wait()
        chunk(k)
    chunk(turns)
    chunk(turns + 1)
    chunk(turns + 2, at1=[lambda: total_loss(0)], at4=[lambda: spread_loss(0)], at5=[lambda: split_sums(0)])
    chunk(
        turns + 3,
        at1=[lambda: total_loss(1)],
        at2=[lambda: gather(0, 0)],
        at3=[lambda: gather(0, 1)],
        at4=[lambda: spread_loss(1), lambda: rank(pairs[0])],
        at5=[lambda: split_sums(1)],
    )
    total_loss(2)
    for t in range(depth):
        price(2 * turns - 1, t * STRIP)
    spread_loss(2)
    gather(1, 0)
    gather(1, 1)
    total_loss(3)
    rank(pairs[1])
    rank(pairs[2])
    spread_loss(3)
    rank(pairs[3])

    rising1 = x >= SIDE // 2
    sign1 = sign_of(rising1)
    target = iota((TOPK, LANES), 0).astype(F32)
    target = jnp.where(rising1, float(TOPK - 1) - target, target)
    chosen = jnp.zeros((TOPK, LANES), F32)
    for b in range(slots // LANES):
        place = jnp.sum(seen[b], axis=0, keepdims=True)
        chosen += jnp.where(place == target, spread[b][0:1], 0.0)
    ordered = jnp.broadcast_to(jnp.sum(chosen, axis=1, keepdims=True) * sign1, (TOPK, LANES))
    for h in range(2):
        list1[0, h:h + 1, :] = along_lanes(ordered[h * LANES:(h + 1) * LANES])

    pl.semaphore_wait(barrier, SIDE - 1 + half - 1)

    def to(src, dst, ssem, rsem, device):
        return pltpu.make_async_remote_copy(
            src_ref=src, dst_ref=dst, send_sem=ssem, recv_sem=rsem,
            device_id={"scen": device}, device_id_type=MESH,
        )

    first = [to(list1.at[0], got1.at[x], send1, recv1, o * half + yc) for o in across]
    cfirst = [to(cand1.at[o], cgot1.at[x], csend1, crecv1, o * half + yc) for o in across]
    for copy in first:
        copy.start()
    got1[x] = list1[0]
    for r in (2, 3):
        split_sums(r)
        gather(r, 0)
        gather(r, 1)
    for m in range(2):
        for t in range(2):
            found = pltpu.matmul_pop(units[m]["gather"][t])
            found = found[0:ENT] + found[ENT:2 * ENT] + found[2 * ENT:3 * ENT]
            for h in range(2):
                cand1[4 * m + 2 * t + h] = found[:, h * LANES:(h + 1) * LANES]

    for copy in cfirst:
        copy.start()
    cgot1[x] = cand1[x]

    def settle(slots_of, others, sem):
        every = slots_of.at[pl.ds(0, others)]
        pltpu.make_async_copy(every, every, sem).wait()

    settle(got1, SIDE - 1, recv1)
    slot = iota((1, LANES), 1)
    all1 = got1[...]
    lists = jnp.concatenate([lists_down(all1[:, h, :]) for h in range(2)], axis=0)
    rising2 = yc >= half // 2
    lists = merge(lists, sign_of((slot & 4) != 0), 4, sign_of((slot & 2) != 0))
    lists = merge(lists, sign_of((slot & 2) != 0), 2, sign_of((slot & 1) != 0))
    lists = merge(lists, sign_of((slot & 1) != 0), 1, sign_of(rising2))
    for h in range(2):
        list2[0, h:h + 1, :] = along_lanes(lists[h * LANES:(h + 1) * LANES])
    second = [to(list2.at[0], got2.at[yc], send2, recv2, x * half + o) for o in along]
    for copy in second:
        copy.start()
    got2[yc] = list2[0]

    settle(cgot1, SIDE - 1, crecv1)
    cand2[0] = jnp.sum(cgot1[...], axis=0)
    csecond = [to(cand2.at[0], cgot2.at[yc], csend2, crecv2, x * half + o) for o in along]
    for copy in csecond:
        copy.start()
    cgot2[yc] = cand2[0]

    settle(got2, half - 1, recv2)
    all2 = got2[...]
    lists = jnp.concatenate([lists_down(all2[:, h, :]) for h in range(2)], axis=0)
    lists = merge(lists, sign_of((slot & 8) != 0), 8, sign_of((slot & 4) != 0))
    lists = merge(lists, sign_of((slot & 4) != 0), 4, sign_of((slot & 2) != 0))
    lists = merge(lists, sign_of((slot & 2) != 0), 2, sign_of((slot & 1) != 0))
    settle(cgot2, half - 1, crecv2)
    summed = jnp.sum(cgot2[...], axis=0)
    flipped[...] = jnp.concatenate([summed] * (LANES // ENT), axis=0).T
    cand_out[...] = flipped[pl.ds(pl.multiple_of(yc * SUB, SUB), SUB), 0:ENT]
    lists = merge(lists, sign_of((slot & 1) != 0), 1, F32(1.0))
    for h in range(2):
        tail_out[h:h + 1, :] = along_lanes(lists[h * LANES:(h + 1) * LANES])

    settle(got1, SIDE - 1, send1)
    settle(cgot1, SIDE - 1, csend1)
    settle(got2, half - 1, send2)
    settle(cgot2, half - 1, csend2)


def kernel(*refs):
    units = []
    for m in range(2):
        total = pltpu.ACC(m)
        units.append({
            "value": [[total((STRIP, TILE), F32)] * (TILE // STRIP)] * 2,
            "sums": total((LANES, TILE), F32),
            "gather": [total((4 * ENT, TILE), F32)] * 2,
        })
    pl.run_scoped(lambda units: search(units, *refs), units)


def body(shocks, factor_sens, notional, moneyness, desk_entity, scenario_counts, candidate_ids):
    slots, factors = shocks.shape
    instruments = factor_sens.shape[1]
    half = SIDE * CORES
    hbm = pl.BlockSpec(memory_space=pltpu.HBM)
    vmem = pl.BlockSpec(memory_space=pltpu.VMEM)
    dma = pltpu.SemaphoreType.DMA
    tail, cand = pl.pallas_call(
        kernel,
        out_shape=(
            pltpu.VMEM((2, LANES), F32),
            pltpu.VMEM((SUB, ENT), F32),
        ),
        in_specs=[pl.BlockSpec(memory_space=pltpu.SMEM)] + [hbm] * 6,
        out_specs=(vmem, vmem),
        scratch_shapes=[
            pltpu.VMEM((slots, factors), BF16),
            pltpu.VMEM((factors, instruments), BF16),
            pltpu.VMEM((SUB, LANES), F32),
            pltpu.VMEM((SUB, LANES), F32),
            pltpu.VMEM((1, K), jnp.int32),
            pltpu.VMEM((SUB, LANES), jnp.int32),
            pltpu.VMEM((SUB, LANES), F32),
            pltpu.VMEM((slots, 2 * TILE), BF16),
            pltpu.VMEM((2 * TILE, TILE), BF16),
            pltpu.VMEM((slots, LANES), F32),
            pltpu.VMEM((slots // LANES, SUB, LANES), F32),
            pltpu.VMEM((slots // LANES, SUB, LANES), F32),
            pltpu.VMEM((slots // LANES, ENT, LANES), F32),
            pltpu.VMEM((4 * ENT, TILE), BF16),
            pltpu.VMEM((1, 2, LANES), F32),
            pltpu.VMEM((1, 2, LANES), F32),
            pltpu.VMEM((SIDE, 2, LANES), F32),
            pltpu.VMEM((half, 2, LANES), F32),
            pltpu.VMEM((SIDE, ENT, LANES), F32),
            pltpu.VMEM((1, ENT, LANES), F32),
            pltpu.VMEM((SIDE, ENT, LANES), F32),
            pltpu.VMEM((half, ENT, LANES), F32),
            pltpu.VMEM((LANES, LANES), F32),
            dma((2 * FIRST + slots // TILE,)),
            dma((4,)),
            dma, dma, dma, dma, dma, dma, dma, dma,
        ],
        compiler_params=pltpu.CompilerParams(
            collective_id=0, has_side_effects=True, vmem_limit_bytes=48 * 1024 * 1024
        ),
        name="tail_search",
    )(
        scenario_counts,
        *[
            pltpu.with_memory_space_constraint(array, pltpu.HBM)
            for array in (
                shocks,
                factor_sens,
                notional.reshape(SUB, LANES),
                moneyness.reshape(SUB, LANES),
                desk_entity.reshape(1, K),
                candidate_ids.reshape(SUB, LANES),
            )
        ],
    )
    return tail.reshape(TOPK), cand


def solution(mesh):
    both = ("grp", "scen")
    return jax.shard_map(
        body,
        mesh=mesh,
        in_specs=(P(both, None), P(), P(), P(), P(), P(both), P("grp")),
        out_specs=(P("grp"), P(both, None)),
        check_vma=False,
    )
```

time: 37.7 us -> 37 us (0.981)
  Pallas kernels: 35.1 us -> 34.5 us
    pallas_call x1, Pallas kernels: 35.1 us -> 34.5 us  [body(): pl.pallas_call(kernel, out_shape=(pltpu.VMEM((2, LANES), F32), pltpu.VMEM...]
where the time goes in v4:
time: 37 us; the launch traced here: 36.9 us
  Pallas kernels  34.5 us (93%)
  between operations  1.29 us (3%)
  local copies, waits for them, and re-layouts  1.16 us (3%)
    pallas_call x1, Pallas kernels, body(): pl.pallas_call(kernel, out_shape=(pltpu.VMEM((2, LANES), F32), pltpu.VMEM...  34.5 us
    unnamed x2, local copies, waits for them, and re-layouts  1.16 us

profile of v4, /device:TPU:515, one launch (start us, length us, event | category | flops | bytes accessed | tf_op | source)
XLA Modules:
  0.0 36.9 jit_solution(17585301990400153137)
XLA Ops:
  1.3 34.5 %tail_search.1 = (f32[2,128]{1,0:T(2,128)S(1)}, f32[8,8]{1,0:T(8,128)S(1)}) custom-call(s32[1]{0:T(128)S(6)} %copy.13.refs_0_, bf16[1024,2048]{1,0:T(8,128)(2,1)} %refs_1_.1, bf16[2048,1024]{1,0:T(8,128)(2,1)} %refs_2_.1, f32[8,128]{1,0:T(8,128)} %bitcast.6, f32[8,128]{1,0:T(8,128)} %bitcast.7, s32[1,64]{1,0:T(1,128)} %bitcast.9, s32[8,128]{1,0:T(8,128)} %bitcast.8), custom_call_target="tpu_custom_call" | custom-call | tf_op jit(solution)/shard_map/tail_search/pallas_call | solution.py:420
  35.8 0.6 %copy.11 = f32[256]{0:T(256)} copy(f32[256]{0:T(256)S(1)} %bitcast.5) | data formatting | bytes 2048
  36.3 0.6 %copy.12 = f32[8,8]{1,0:T(8,128)} copy(f32[8,8]{1,0:T(8,128)S(1)} %get-tuple-element.7) | data formatting | bytes 512

commit v5 on v4

--- a/solution.py
+++ b/solution.py
@@ -108,7 +108,8 @@
             rows = pl.ds(r * TILE, TILE)
             return copy_in(shocks.at[rows], sh.at[rows], 2 * FIRST + r)
         if n == "right":
-            return copy_in(part(sens, 0, factors, wide, wide), part(fs, 0, factors, wide, wide), 2 * FIRST)
+            where = (r * factors // 2, factors // 2, wide, wide)
+            return copy_in(part(sens, *where), part(fs, *where), 2 * FIRST + (r and turns))
         at = n % FIRST * deep
         if n < FIRST:
             where = (0, TILE, at, deep)
@@ -122,20 +123,25 @@
             [(moneyness, mv), (notional, nv), (desk_entity, dv), (ids, iv)]
         )
     ]
-    for n in range(FIRST):
+    def start_piece(n):
         load(n).start()
         load(FIRST + n).start()
+
+    start_piece(0)
     for copy in small:
         copy.start()
-    for r in range(1, turns):
-        load("rows", r).start()
-    load("right").start()
 
     barrier = pltpu.get_barrier_semaphore()
-    for other in across:
-        pl.semaphore_signal(barrier, inc=1, device_id={"scen": other * half + yc}, device_id_type=MESH)
-    for other in along:
-        pl.semaphore_signal(barrier, inc=1, device_id={"scen": x * half + other}, device_id_type=MESH)
+    greeted = [other * half + yc for other in across] + [x * half + other for other in along]
+    for n, other in enumerate(greeted):
+        pl.semaphore_signal(barrier, inc=1, device_id={"scen": other}, device_id_type=MESH)
+        if n == 4:
+            start_piece(1)
+        if n == 10:
+            start_piece(2)
+        if n == 16:
+            start_piece(3)
+    load("rows", 1).start()
 
     for copy in small:
         copy.wait()
@@ -267,6 +273,8 @@
             for i in (*old, *blocks):
                 compare(i, b)
 
+    following = [[load("rows", 2)], [load("rows", 3)], [load("right", 0)], [load("right", 1)]]
+
     def chunk(k, **work):
         @pl.when(me >= 0)
         def _():
@@ -274,9 +282,13 @@
                 if k == 0 and t % 2 == 0:
                     load(t // 2).wait()
                     load(FIRST + t // 2).wait()
+                    for copy in following[t // 2]:
+                        copy.start()
                     stage(t)
                 if k == turns - 1 and t == depth - 1:
-                    load("right").wait()
+                    load("right", 0).wait()
+                if k == turns and t == depth // 2 - 1:
+                    load("right", 1).wait()
                 step(k * depth + t, k == 0 and t % 2 == 1)
                 if k > 0:
                     price(k - 1, t * STRIP)
@@ -291,21 +303,19 @@
         chunk(k)
     chunk(turns)
     chunk(turns + 1)
-    chunk(turns + 2, at1=[lambda: total_loss(0)], at4=[lambda: spread_loss(0)], at5=[lambda: split_sums(0)])
+    chunk(turns + 2, at4=[lambda: total_loss(0)], at7=[lambda: spread_loss(0), lambda: split_sums(0)])
     chunk(
         turns + 3,
-        at1=[lambda: total_loss(1)],
+        at1=[lambda: rank(pairs[0])],
         at2=[lambda: gather(0, 0)],
         at3=[lambda: gather(0, 1)],
-        at4=[lambda: spread_loss(1), lambda: rank(pairs[0])],
-        at5=[lambda: split_sums(1)],
+        at5=[lambda: total_loss(1)],
     )
+    spread_loss(1)
     total_loss(2)
     for t in range(depth):
         price(2 * turns - 1, t * STRIP)
     spread_loss(2)
-    gather(1, 0)
-    gather(1, 1)
     total_loss(3)
     rank(pairs[1])
     rank(pairs[2])
@@ -337,7 +347,7 @@
     for copy in first:
         copy.start()
     got1[x] = list1[0]
-    for r in (2, 3):
+    for r in range(1, turns):
         split_sums(r)
         gather(r, 0)
         gather(r, 1)
@@ -408,6 +418,17 @@
             "gather": [total((4 * ENT, TILE), F32)] * 2,
         })
     pl.run_scoped(lambda units: search(units, *refs), units)
+
+
+def store(tail, cand, tail_out, cand_out, sems):
+    copies = [
+        pltpu.make_async_copy(tail, tail_out, sems.at[0]),
+        pltpu.make_async_copy(cand, cand_out, sems.at[1]),
+    ]
+    for copy in copies:
+        copy.start()
+    for copy in copies:
+        copy.wait()
 
 
 def body(shocks, factor_sens, notional, moneyness, desk_entity, scenario_counts, candidate_ids):
@@ -449,7 +470,7 @@
             pltpu.VMEM((SIDE, ENT, LANES), F32),
             pltpu.VMEM((half, ENT, LANES), F32),
             pltpu.VMEM((LANES, LANES), F32),
-            dma((2 * FIRST + slots // TILE,)),
+            dma((2 * FIRST + slots // TILE + 1,)),
             dma((4,)),
             dma, dma, dma, dma, dma, dma, dma, dma,
         ],
@@ -471,6 +492,14 @@
             )
         ],
     )
+    tail, cand = pl.pallas_call(
+        store,
+        out_shape=(pltpu.HBM((2, LANES), F32), pltpu.HBM((SUB, ENT), F32)),
+        in_specs=[vmem, vmem],
+        out_specs=(hbm, hbm),
+        scratch_shapes=[dma((2,))],
+        name="store",
+    )(*[pltpu.with_memory_space_constraint(array, pltpu.VMEM) for array in (tail, cand)])
     return tail.reshape(TOPK), cand
 
 

time: 37 us -> 35.3 us (0.954)
  local copies, waits for them, and re-layouts: 1.16 us -> 0 us
  Pallas kernels: 34.5 us -> 33.8 us
    pallas_call x1, Pallas kernels: 34.5 us -> 33.2 us  [body(): pl.pallas_call(kernel, out_shape=(pltpu.VMEM((2, LANES), F32), pltpu.VMEM...]
    unnamed x2 -> x0, local copies, waits for them, and re-layouts: 1.16 us -> none
    pallas_call x0 -> x1, Pallas kernels: none -> 0.62 us  [body(): pl.pallas_call(store, out_shape=(pltpu.HBM((2, LANES), F32), pltpu.HBM((S...]
where the time goes in v5:
time: 35.3 us; the launch traced here: 35.1 us
  Pallas kernels  33.8 us (96%)
  between operations  1.29 us (4%)
    pallas_call x1, Pallas kernels, body(): pl.pallas_call(kernel, out_shape=(pltpu.VMEM((2, LANES), F32), pltpu.VMEM...  33.2 us

profile of v5, /device:TPU:515, one launch (start us, length us, event | category | flops | bytes accessed | tf_op | source)
XLA Modules:
  0.0 35.1 jit_solution(5053997534995381024)
XLA Ops:
  1.3 33.2 %tail_search.1 = (f32[2,128]{1,0:T(2,128)S(1)}, f32[8,8]{1,0:T(8,128)S(1)}) custom-call(s32[1]{0:T(128)S(6)} %copy.9.refs_0_, bf16[1024,2048]{1,0:T(8,128)(2,1)} %refs_1_.1, bf16[2048,1024]{1,0:T(8,128)(2,1)} %refs_2_.1, f32[8,128]{1,0:T(8,128)} %bitcast.5, f32[8,128]{1,0:T(8,128)} %bitcast.6, s32[1,64]{1,0:T(1,128)} %bitcast.8, s32[8,128]{1,0:T(8,128)} %bitcast.7), custom_call_target="tpu_custom_call" | custom-call | tf_op jit(solution)/shard_map/tail_search/pallas_call | solution.py:441
  34.5 0.6 %store.1 = (f32[2,128]{1,0:T(2,128)}, f32[8,8]{1,0:T(8,128)}) custom-call(f32[2,128]{1,0:T(2,128)S(1)} %get-tuple-element.6.tail, f32[8,8]{1,0:T(8,128)S(1)} %get-tuple-element.7.cand), custom_call_target="tpu_custom_call" | custom-call | tf_op jit(solution)/shard_map/store/pallas_call | solution.py:495

commit v6 on v5

--- a/solution.py
+++ b/solution.py
@@ -58,11 +58,9 @@
     at = iota(y.shape, 1)
     for stride in (4, 2, 1):
         low = (at & stride) == 0
-        if stride == 4:
-            other = pltpu.roll(y, 4, 1)
-        else:
-            other = jnp.where(low, pltpu.roll(y, SUB - stride, 1), pltpu.roll(y, stride, 1))
-        y = jnp.where(low, jnp.maximum(y, other), jnp.minimum(y, other))
+        later = pltpu.roll(y, SUB - stride, 1)
+        earlier = later if stride == 4 else pltpu.roll(y, stride, 1)
+        y = jnp.where(low, jnp.maximum(y, later), jnp.minimum(y, earlier))
     return y.reshape(TOPK, LANES)
 
 
@@ -84,7 +82,7 @@
     units, cv, shocks, sens, notional, moneyness, desk_entity, ids,
     tail_out, cand_out,
     sh, fs, nv, mv, dv, iv, base_soft, terms, indicator, column, spread, seen, by_entity, split,
-    list1, list2, got1, got2, cand1, cand2, cgot1, cgot2, flipped,
+    list1, list2, got1, got2, cand1, cand2, cgot1, cgot2,
     load_sem, small_sem, send1, recv1, send2, recv2, csend1, crecv1, csend2, crecv2,
 ):
     slots, factors = sh.shape
@@ -303,15 +301,13 @@
         chunk(k)
     chunk(turns)
     chunk(turns + 1)
-    chunk(turns + 2, at4=[lambda: total_loss(0)], at7=[lambda: spread_loss(0), lambda: split_sums(0)])
+    chunk(turns + 2, at4=[lambda: total_loss(0)], at7=[lambda: spread_loss(0)])
     chunk(
         turns + 3,
         at1=[lambda: rank(pairs[0])],
-        at2=[lambda: gather(0, 0)],
-        at3=[lambda: gather(0, 1)],
-        at5=[lambda: total_loss(1)],
+        at3=[lambda: total_loss(1)],
+        at6=[lambda: spread_loss(1)],
     )
-    spread_loss(1)
     total_loss(2)
     for t in range(depth):
         price(2 * turns - 1, t * STRIP)
@@ -347,7 +343,7 @@
     for copy in first:
         copy.start()
     got1[x] = list1[0]
-    for r in range(1, turns):
+    for r in range(turns):
         split_sums(r)
         gather(r, 0)
         gather(r, 1)
@@ -382,11 +378,15 @@
     got2[yc] = list2[0]
 
     settle(cgot1, SIDE - 1, crecv1)
-    cand2[0] = jnp.sum(cgot1[...], axis=0)
-    csecond = [to(cand2.at[0], cgot2.at[yc], csend2, crecv2, x * half + o) for o in along]
+    turned = jnp.concatenate([jnp.sum(cgot1[...], axis=0)] * (LANES // ENT), axis=0).T
+    own_lanes = iota((SUB, LANES), 1) // ENT == iota((SUB, LANES), 0)
+    for o in range(half):
+        mine = jnp.where(own_lanes, turned[o * SUB:(o + 1) * SUB], 0.0)
+        cand2[o] = jnp.sum(mine, axis=0, keepdims=True)
+    csecond = [to(cand2.at[o], cgot2.at[yc], csend2, crecv2, x * half + o) for o in along]
     for copy in csecond:
         copy.start()
-    cgot2[yc] = cand2[0]
+    cgot2[yc] = cand2[yc]
 
     settle(got2, half - 1, recv2)
     all2 = got2[...]
@@ -395,9 +395,11 @@
     lists = merge(lists, sign_of((slot & 4) != 0), 4, sign_of((slot & 2) != 0))
     lists = merge(lists, sign_of((slot & 2) != 0), 2, sign_of((slot & 1) != 0))
     settle(cgot2, half - 1, crecv2)
-    summed = jnp.sum(cgot2[...], axis=0)
-    flipped[...] = jnp.concatenate([summed] * (LANES // ENT), axis=0).T
-    cand_out[...] = flipped[pl.ds(pl.multiple_of(yc * SUB, SUB), SUB), 0:ENT]
+    summed = jnp.broadcast_to(jnp.sum(cgot2[...], axis=0), (SUB, LANES))
+    by_row = summed
+    for q in range(1, SUB):
+        by_row = jnp.where(iota((SUB, LANES), 0) == q, pltpu.roll(summed, LANES - q * ENT, 1), by_row)
+    cand_out[...] = by_row[:, 0:ENT]
     lists = merge(lists, sign_of((slot & 1) != 0), 1, F32(1.0))
     for h in range(2):
         tail_out[h:h + 1, :] = along_lanes(lists[h * LANES:(h + 1) * LANES])
@@ -466,10 +468,9 @@
             pltpu.VMEM((SIDE, 2, LANES), F32),
             pltpu.VMEM((half, 2, LANES), F32),
             pltpu.VMEM((SIDE, ENT, LANES), F32),
-            pltpu.VMEM((1, ENT, LANES), F32),
+            pltpu.VMEM((half, 1, LANES), F32),
             pltpu.VMEM((SIDE, ENT, LANES), F32),
-            pltpu.VMEM((half, ENT, LANES), F32),
-            pltpu.VMEM((LANES, LANES), F32),
+            pltpu.VMEM((half, 1, LANES), F32),
             dma((2 * FIRST + slots // TILE + 1,)),
             dma((4,)),
             dma, dma, dma, dma, dma, dma, dma, dma,

time: 35.3 us -> 35.1 us (level)
  no operation moved by 1% of the time
where the time goes in v6:
time: 35.1 us; the launch traced here: 35 us
  Pallas kernels  33.7 us (96%)
  between operations  1.29 us (4%)
    pallas_call x1, Pallas kernels, body(): pl.pallas_call(kernel, out_shape=(pltpu.VMEM((2, LANES), F32), pltpu.VMEM...  33.1 us

profile of v6, /device:TPU:515, one launch (start us, length us, event | category | flops | bytes accessed | tf_op | source)
XLA Modules:
  0.0 35.0 jit_solution(6802443741016785041)
XLA Ops:
  1.3 33.1 %tail_search.1 = (f32[2,128]{1,0:T(2,128)S(1)}, f32[8,8]{1,0:T(8,128)S(1)}) custom-call(s32[1]{0:T(128)S(6)} %copy.9.refs_0_, bf16[1024,2048]{1,0:T(8,128)(2,1)} %refs_1_.1, bf16[2048,1024]{1,0:T(8,128)(2,1)} %refs_2_.1, f32[8,128]{1,0:T(8,128)} %bitcast.5, f32[8,128]{1,0:T(8,128)} %bitcast.6, s32[1,64]{1,0:T(1,128)} %bitcast.8, s32[8,128]{1,0:T(8,128)} %bitcast.7), custom_call_target="tpu_custom_call" | custom-call | tf_op jit(solution)/shard_map/tail_search/pallas_call | solution.py:443
  34.4 0.6 %store.1 = (f32[2,128]{1,0:T(2,128)}, f32[8,8]{1,0:T(8,128)}) custom-call(f32[2,128]{1,0:T(2,128)S(1)} %get-tuple-element.6.tail, f32[8,8]{1,0:T(8,128)S(1)} %get-tuple-element.7.cand), custom_call_target="tpu_custom_call" | custom-call | tf_op jit(solution)/shard_map/store/pallas_call | solution.py:496

commit v7 on v6

--- a/solution.py
+++ b/solution.py
@@ -47,9 +47,10 @@
     return jnp.where(low, up, down)
 
 
-def merge(stored, own, step, after):
+def merge(stored, own, step, after, met=None):
     value = stored * own
-    x = jnp.maximum(value, pltpu.roll(value, step, 1)) * after
+    other = pltpu.roll(value, step, 1) if met is None else -(met * own)
+    x = jnp.maximum(value, other) * after
     for stride in (128, 64, 32, 16, 8):
         y = x.reshape(TOPK // (2 * stride), 2, stride, LANES)
         a, b = y[:, 0], y[:, 1]
@@ -67,6 +68,11 @@
 def lists_down(rows):
     copies = LANES // rows.shape[0]
     return jnp.concatenate([rows] * copies, axis=0).T
+
+
+def halves_swapped(rows):
+    middle = rows.shape[0] // 2
+    return jnp.concatenate([rows[middle:], rows[:middle]], axis=0)
 
 
 def along_lanes(column):
@@ -366,8 +372,9 @@
     slot = iota((1, LANES), 1)
     all1 = got1[...]
     lists = jnp.concatenate([lists_down(all1[:, h, :]) for h in range(2)], axis=0)
+    met = jnp.concatenate([lists_down(halves_swapped(all1[:, h, :])) for h in range(2)], axis=0)
     rising2 = yc >= half // 2
-    lists = merge(lists, sign_of((slot & 4) != 0), 4, sign_of((slot & 2) != 0))
+    lists = merge(lists, sign_of((slot & 4) != 0), 4, sign_of((slot & 2) != 0), met)
     lists = merge(lists, sign_of((slot & 2) != 0), 2, sign_of((slot & 1) != 0))
     lists = merge(lists, sign_of((slot & 1) != 0), 1, sign_of(rising2))
     for h in range(2):
@@ -391,7 +398,8 @@
     settle(got2, half - 1, recv2)
     all2 = got2[...]
     lists = jnp.concatenate([lists_down(all2[:, h, :]) for h in range(2)], axis=0)
-    lists = merge(lists, sign_of((slot & 8) != 0), 8, sign_of((slot & 4) != 0))
+    met = jnp.concatenate([lists_down(halves_swapped(all2[:, h, :])) for h in range(2)], axis=0)
+    lists = merge(lists, sign_of((slot & 8) != 0), 8, sign_of((slot & 4) != 0), met)
     lists = merge(lists, sign_of((slot & 4) != 0), 4, sign_of((slot & 2) != 0))
     lists = merge(lists, sign_of((slot & 2) != 0), 2, sign_of((slot & 1) != 0))
     settle(cgot2, half - 1, crecv2)

time: 35.1 us -> 35 us (level)
  no operation moved by 1% of the time
where the time goes in v7:
time: 35 us; the launch traced here: 34.9 us
  Pallas kernels  33.6 us (96%)
  between operations  1.29 us (4%)
    pallas_call x1, Pallas kernels, body(): pl.pallas_call(kernel, out_shape=(pltpu.VMEM((2, LANES), F32), pltpu.VMEM...  33 us

profile of v7, /device:TPU:515, one launch (start us, length us, event | category | flops | bytes accessed | tf_op | source)
XLA Modules:
  0.0 34.9 jit_solution(7729520516133349231)
XLA Ops:
  1.3 33.0 %tail_search.1 = (f32[2,128]{1,0:T(2,128)S(1)}, f32[8,8]{1,0:T(8,128)S(1)}) custom-call(s32[1]{0:T(128)S(6)} %copy.9.refs_0_, bf16[1024,2048]{1,0:T(8,128)(2,1)} %refs_1_.1, bf16[2048,1024]{1,0:T(8,128)(2,1)} %refs_2_.1, f32[8,128]{1,0:T(8,128)} %bitcast.5, f32[8,128]{1,0:T(8,128)} %bitcast.6, s32[1,64]{1,0:T(1,128)} %bitcast.8, s32[8,128]{1,0:T(8,128)} %bitcast.7), custom_call_target="tpu_custom_call" | custom-call | tf_op jit(solution)/shard_map/tail_search/pallas_call | solution.py:451
  34.3 0.6 %store.1 = (f32[2,128]{1,0:T(2,128)}, f32[8,8]{1,0:T(8,128)}) custom-call(f32[2,128]{1,0:T(2,128)S(1)} %get-tuple-element.6.tail, f32[8,8]{1,0:T(8,128)S(1)} %get-tuple-element.7.cand), custom_call_target="tpu_custom_call" | custom-call | tf_op jit(solution)/shard_map/store/pallas_call | solution.py:504
